TPU v7x, 32 devices: a whole 2x2x4 slice. The times are simulated.
32 devices in a mesh: row: 8 (over z, core), col: 4 (over y, x).
Axes of the slice: x: 2, y: 2, z: 4, core: 2. Of those that a mesh axis runs over, the one named last changes fastest.
Arguments:
- attn_out: bfloat16 [6, 512, 2048], P(None, 'col', 'row'), may hold values from -0.625 to 0.625
- out_cotangent: bfloat16 [6, 512, 2048], P(None, 'row', 'col'), may hold values from -6 to 6
- frozen: bfloat16 [6, 2048, 2048], P(None, 'row', 'col'), may hold values from -0.5 to 0.5
- adapt_in: bfloat16 [6, 32, 2048], P(None, None, 'row'), may hold values from -0.125 to 0.125
- adapt_out: bfloat16 [6, 32, 2048], P(None, None, 'col'), may hold values from -1 to 1
- magnitude: float32 [6, 2048], P(None, 'col'), may hold values from 0.1 to 1.9
Outputs:
- input_grad: bfloat16 [6, 512, 2048], P(None, 'col', 'row')
- adapt_in_grad: float32 [6, 32, 2048], P(None, None, 'row')
- adapt_out_grad: float32 [6, 32, 2048], P(None, None, 'col')
- magnitude_grad: float32 [6, 2048], P(None, 'col')
All inputs are finite; a program needn't handle non-finite values.
Results may differ from a plain program's by a relative error of at most 0.0065.
Values may be sent and summed in bfloat16 or wider, within the bound.
A program may use at most 64 MiB of HBM per device.

v0:
```python
import functools

import jax
import jax.numpy as jnp
from jax import lax
from jax.experimental import pallas as pl
from jax.experimental.pallas import tpu as pltpu
from jax.sharding import PartitionSpec as P

MESH = pl.DeviceIdType.MESH
F32 = jnp.float32
BF16 = jnp.bfloat16


def mm(a, b, dims):
    return lax.dot_general(a, b, (dims, ((), ())), preferred_element_type=F32)


def kernel(
    R, C,
    acts_hbm, grads_hbm, frozen_hbm, ain_hbm, aout_hbm, mag_hbm,
    ig_hbm, ing_hbm, oug_hbm, mgrad_hbm,
    acts, grads, frozen, ain, aout, mag,
    ig, ing, oug, mgrad, load, save,
    G, A, merged, wlow, prod, own, rs_send, rs_recv,
    sq, dt, im_send, im_sib, im_acc, im_recv, io_send, io_sib, io_acc, io_recv, og, q, q_recv,
    scl, cor, mag3, send, g_in, g_fw, a_in, rs_in, sq_in, dt_in, im_in, io_in, io_fw, og_in, og_fw, q_in,
):
    pairs = ((grads_hbm, grads), (acts_hbm, acts), (frozen_hbm, frozen),
             (ain_hbm, ain), (aout_hbm, aout), (mag_hbm, mag))
    loads = [pltpu.make_async_copy(a, b, load.at[i]) for i, (a, b) in enumerate(pairs)]
    for copy in loads:
        copy.start()
    pairs = ((mgrad, mgrad_hbm), (ig, ig_hbm), (ing, ing_hbm), (oug, oug_hbm))
    saves = [pltpu.make_async_copy(a, b, save.at[i]) for i, (a, b) in enumerate(pairs)]
    L, TR, W = grads.shape
    TC, KI = acts.shape[1:]
    RANK = ain.shape[1]
    k = RANK // R
    Z = R // 2
    ahead = min(4, L)
    r, c = lax.axis_index("row"), lax.axis_index("col")
    z, core = r // 2, lax.rem(r, 2)
    sib = 2 * z + 1 - core

    def row_to(d):
        return lax.rem(r + d, R)

    def row_from(d):
        return lax.rem(r + R - d, R)

    def col_to(d):
        return lax.rem(c + d, C)

    def z_to(d):
        return 2 * lax.rem(z + d, Z) + core

    def z_from(d):
        return 2 * lax.rem(z + Z - d, Z) + core

    def rows(at, size):
        return pl.ds(pl.multiple_of(at * size, size), size)

    def rcopy(src, dst, cat, recv, **dev):
        return pltpu.make_async_remote_copy(
            src_ref=src, dst_ref=dst, send_sem=send.at[cat], recv_sem=recv,
            device_id=dev, device_id_type=MESH,
        )

    barrier = pltpu.get_barrier_semaphore()
    for d in range(1, R):
        pl.semaphore_signal(barrier, inc=1, device_id={"row": row_to(d)}, device_id_type=MESH)
    for d in range(1, C):
        pl.semaphore_signal(barrier, inc=1, device_id={"col": col_to(d)}, device_id_type=MESH)
    pl.semaphore_wait(barrier, R + C - 2)

    def g_block(l, at, which):
        return G.at[l, rows(2 * at + which, TR)]

    def g_own(l, step):
        if step == 0:
            return rcopy(grads.at[l], g_block(l, z, core), 2, g_fw.at[l, z], row=sib)
        return rcopy(grads.at[l], g_block(l, z, core), 0, g_in.at[l, z], row=r + 2 * step)

    def g_pass(l, at, step):
        block = g_block(l, at, core)
        if step == 0:
            return rcopy(block, block, 2, g_fw.at[l, at], row=sib)
        return rcopy(block, block, 0, g_in.at[l, at], row=r + 2 * step)

    def g_own_each(l, act):
        act(g_own(l, 0))

        @pl.when(z < Z - 1)
        def _():
            act(g_own(l, 1))

        @pl.when(z > 0)
        def _():
            act(g_own(l, -1))

    def g_relay(l, d, act, arrive):
        for step in (1, -1):
            at = z - step * d

            @pl.when(jnp.logical_and(at >= 0, at < Z))
            def _():
                if arrive:
                    rcopy(grads.at[l], g_block(l, at, core), 0, g_in.at[l, at], row=r).wait_recv()

                @pl.when(jnp.logical_and(z + step >= 0, z + step < Z))
                def _():
                    act(g_pass(l, at, step))

                act(g_pass(l, at, 0))

    def a_copy(l, d):
        return rcopy(acts.at[l], A.at[l, rows(c, TC)], 1, a_in.at[l, d], col=col_to(d))

    def rs_copy(l, d):
        return rcopy(rs_send.at[d, l], rs_recv.at[d, l], 3, rs_in.at[l, d], col=col_to(d))

    def sq_copy(d):
        return rcopy(sq.at[r], sq.at[r], 4, sq_in.at[d], row=row_to(d))

    def dt_copy(l, d):
        return rcopy(dt.at[r, l], dt.at[r, l], 5, dt_in.at[l, d], row=row_to(d))

    def at_z(d):
        return lax.rem(z + d, Z)

    def im_copy(d):
        if d == 0:
            return rcopy(im_send.at[1 - core], im_sib, 6, im_in.at[0], row=sib)
        return rcopy(im_acc.at[at_z(d)], im_recv.at[z], 7, im_in.at[d], row=z_to(d))

    def io_fw_copy(l):
        return rcopy(io_send.at[1 - core, l], io_sib.at[l], 8, io_fw.at[l], row=sib)

    def io_copy(l, d):
        return rcopy(io_acc.at[at_z(d), l], io_recv.at[z, l], 9, io_in.at[l, d], row=z_to(d))

    def og_copy(d):
        return rcopy(og.at[r], og.at[r], 11, og_in.at[d], row=sib if d == 0 else z_to(d))

    def og_fw_copy(d):
        return rcopy(og.at[z_from(d)], og.at[z_from(d)], 12, og_fw.at[d], row=sib)

    def q_copy(d):
        return rcopy(q, q_recv.at[d], 10, q_in.at[d], col=col_to(d))

    loads[0].wait()
    loads[1].wait()

    @pl.loop(0, L)
    def _(l):
        @pl.when(l < ahead)
        def _():
            g_own_each(l, lambda copy: copy.start())

        for d in range(1, C):
            a_copy(l, d).start()

    for copy in loads[2:]:
        copy.wait()

    @pl.loop(0, L)
    def _(l):
        G[l, rows(r, TR)] = grads[l]
        A[l, rows(c, TC)] = acts[l]
        m = frozen[l].astype(F32) + mm(ain[l], aout[l], ((0,), (0,)))
        merged[l] = m
        low = m.astype(BF16)
        wlow[l] = low
        sq[r, l] = jnp.sum(m * m, axis=0, keepdims=True)
        inner = mm(ain[l], low, ((1,), (0,)))
        for s in range(R):
            im_send[s % 2, s // 2, l] = inner[s * k:(s + 1) * k]

    for d in range(1, R):
        sq_copy(d).start()
    im_copy(0).start()
    for l in range(L):
        mag3[l] = mag[l:l + 1]
    if ahead < L:
        g_own_each(ahead, lambda copy: copy.start())

    def scales_ready():
        for d in range(1, R):
            rcopy(sq.at[r], sq.at[row_from(d)], 4, sq_in.at[d], row=r).wait_recv()
        total = sq[0]
        for s in range(1, R):
            total = total + sq[s]
        norms = jnp.sqrt(total + 0.25)
        cor[...] = norms
        scl[...] = mag3[...] / norms

    def pass_on(l):
        rcopy(io_sib.at[l], io_sib.at[l], 8, io_fw.at[l], row=sib).wait_recv()
        for s in range(Z):
            io_acc[s, l] = io_send[core, l, s] + io_sib[l, s]
        for d in range(1, Z):
            io_copy(l, d).start()
        io_recv[z, l] = io_acc[z, l]

    def compute(l):
        for at in range(Z):
            rcopy(grads.at[l], g_block(l, at, 1 - core), 2, g_fw.at[l, at], row=r).wait_recv()
        scale = scl[l]
        g = G[l]
        scaled = (g.astype(F32) * scale).astype(BF16)
        prod[...] = mm(scaled, wlow[l], ((1,), (1,)))
        for d in range(1, C):
            rs_send[d, l] = prod[rows(col_to(d), TC)].astype(BF16)
            rs_copy(l, d).start()
        own[l] = prod[rows(c, TC)]
        for d in range(1, C):
            src = lax.rem(c + C - d, C)
            rcopy(acts.at[l], A.at[l, rows(src, TC)], 1, a_in.at[l, d], col=c).wait_recv()
        outer = mm(A[l], g, ((0,), (0,)))
        dt[r, l] = jnp.sum(merged[l] * outer, axis=0, keepdims=True)
        for d in range(1, R):
            dt_copy(l, d).start()
        inner = mm(ain[l], outer.astype(BF16), ((1,), (0,)))
        for s in range(R):
            io_send[s % 2, l, s // 2] = inner[s * k:(s + 1) * k]
        io_fw_copy(l).start()

        @pl.when(l > 0)
        def _():
            pass_on(l - 1)

        ing[l] = mm(aout[l], (outer * scale).astype(BF16), ((1,), (1,)))

    @pl.loop(0, L + Z - 1)
    def _(at):
        @pl.when(at + ahead + 1 < L)
        def _():
            g_own_each(at + ahead + 1, lambda copy: copy.start())

        for d in range(1, Z):
            l = at - (d - 1)

            @pl.when(jnp.logical_and(l >= 0, l < L))
            def _():
                g_relay(l, d, lambda copy: copy.start(), True)

        @pl.when(at == L + Z - 3)
        def _():
            im_copy(0).wait_recv()
            im_acc[...] = im_send[core] + im_sib[...]
            for d in range(1, Z):
                im_copy(d).start()
            im_recv[z] = im_acc[z]

        @pl.when(at == Z - 1)
        def _():
            scales_ready()

        @pl.when(at >= Z - 1)
        def _():
            compute(at - (Z - 1))

    pass_on(L - 1)

    @pl.loop(0, L)
    def _(l):
        for d in range(1, R):
            rcopy(dt.at[r, l], dt.at[row_from(d), l], 5, dt_in.at[l, d], row=r).wait_recv()

    dots = dt[0]
    for s in range(1, R):
        dots = dots + dt[s]
    norms = cor[...]
    ratio = dots / norms
    for l in range(L):
        mgrad[l:l + 1] = ratio[l]
    saves[0].start()
    cor[...] = -mag3[...] * dots / (norms * norms * norms)

    @pl.loop(0, L)
    def _(l):
        adjusted = (merged[l] * cor[l]).astype(BF16)
        part = ing[l] + mm(aout[l], adjusted, ((1,), (1,)))
        ing[l] = part
        q[l] = part.astype(BF16)

    for d in range(1, C):
        q_copy(d).start()
    for d in range(1, Z):
        src = lax.rem(z + Z - d, Z)
        rcopy(im_recv.at[z], im_recv.at[src], 7, im_in.at[d], row=r).wait_recv()

    @pl.loop(0, L)
    def _(l):
        for d in range(1, Z):
            src = lax.rem(z + Z - d, Z)
            rcopy(io_recv.at[z, l], io_recv.at[src, l], 9, io_in.at[l, d], row=r).wait_recv()
        summed, side = io_recv[0, l], im_recv[0, l]
        for s in range(1, Z):
            summed = summed + io_recv[s, l]
            side = side + im_recv[s, l]
        og[r, l] = summed * scl[l] + side * cor[l]

    for d in range(Z):
        og_copy(d).start()

    @pl.loop(0, L)
    def _(l):
        result = own[l]
        for d in range(1, C):
            rcopy(rs_send.at[d, l], rs_recv.at[d, l], 3, rs_in.at[l, d], col=c).wait_recv()
            result = result + rs_recv[d, l].astype(F32)
        ig[l] = result.astype(BF16)

    saves[1].start()

    for d in range(1, C):
        rcopy(q, q_recv.at[d], 10, q_in.at[d], col=c).wait_recv()

    @pl.loop(0, L)
    def _(l):
        result = ing[l]
        for d in range(1, C):
            result = result + q_recv[d, l].astype(F32)
        ing[l] = result

    saves[2].start()

    for d in range(1, Z):
        rcopy(og.at[r], og.at[z_from(d)], 11, og_in.at[d], row=r).wait_recv()
        og_fw_copy(d).start()
    rcopy(og.at[r], og.at[sib], 11, og_in.at[0], row=r).wait_recv()
    for d in range(1, Z):
        from_sib = 2 * lax.rem(z + Z - d, Z) + 1 - core
        rcopy(og.at[r], og.at[from_sib], 12, og_fw.at[d], row=r).wait_recv()

    @pl.loop(0, L)
    def _(l):
        for s in range(R):
            oug[l, s * k:(s + 1) * k] = og[s, l]

    saves[3].start()

    @pl.loop(0, L)
    def _(l):
        g_own_each(l, lambda copy: copy.wait_send())
        for d in range(1, Z):
            g_relay(l, d, lambda copy: copy.wait_send(), False)
        for d in range(1, C):
            a_copy(l, d).wait_send()
            rs_copy(l, d).wait_send()

    @pl.loop(0, L)
    def _(l):
        for d in range(1, R):
            dt_copy(l, d).wait_send()
        io_fw_copy(l).wait_send()
        for d in range(1, Z):
            io_copy(l, d).wait_send()

    for d in range(1, R):
        sq_copy(d).wait_send()
    for d in range(Z):
        im_copy(d).wait_send()
        og_copy(d).wait_send()
    for d in range(1, Z):
        og_fw_copy(d).wait_send()
    for d in range(1, C):
        q_copy(d).wait_send()
    for copy in saves:
        copy.wait()


def finish(ig, ing, oug, mgrad, ig_out, ing_out, oug_out, mgrad_out):
    ig_out[...] = ig[...]
    ing_out[...] = ing[...]
    oug_out[...] = oug[...]
    mgrad_out[...] = mgrad[...]


def body(R, C, acts, grads, frozen, ain, aout, mag):
    L, TR, W = grads.shape
    TC, KI = acts.shape[1:]
    RANK = ain.shape[1]
    k, T, Z = RANK // R, TR * R, R // 2
    V = pltpu.VMEM
    dma = pltpu.SemaphoreType.DMA
    vm = pl.BlockSpec(memory_space=pltpu.VMEM)
    hbm = pl.BlockSpec(memory_space=pltpu.HBM)
    ig, ing, oug, mgrad = pl.pallas_call(
        functools.partial(kernel, R, C),
        out_shape=(
            jax.ShapeDtypeStruct((L, TC, KI), BF16),
            jax.ShapeDtypeStruct((L, RANK, KI), F32),
            jax.ShapeDtypeStruct((L, RANK, W), F32),
            jax.ShapeDtypeStruct((L, W), F32),
        ),
        in_specs=[hbm] * 6,
        out_specs=(hbm,) * 4,
        scratch_shapes=[
            V(acts.shape, BF16), V(grads.shape, BF16), V(frozen.shape, BF16),
            V(ain.shape, BF16), V(aout.shape, BF16), V(mag.shape, F32),
            V((L, TC, KI), BF16), V((L, RANK, KI), F32), V((L, RANK, W), F32), V((L, W), F32),
            dma((6,)), dma((4,)),
            V((L, T, W), BF16), V((L, T, KI), BF16), V((L, KI, W), F32), V((L, KI, W), BF16),
            V((T, KI), F32), V((L, TC, KI), F32), V((C, L, TC, KI), BF16), V((C, L, TC, KI), BF16),
            V((R, L, 1, W), F32), V((R, L, 1, W), F32),
            V((2, Z, L, k, W), F32), V((Z, L, k, W), F32), V((Z, L, k, W), F32), V((Z, L, k, W), F32),
            V((2, L, Z, k, W), F32), V((L, Z, k, W), F32), V((Z, L, k, W), F32), V((Z, L, k, W), F32),
            V((R, L, k, W), F32), V((L, RANK, KI), BF16), V((C, L, RANK, KI), BF16),
            V((L, 1, W), F32), V((L, 1, W), F32), V((L, 1, W), F32),
            dma((13,)), dma((L, Z)), dma((L, Z)), dma((L, C)), dma((L, C)),
            dma((R,)), dma((L, R)), dma((Z,)), dma((L, Z)), dma((L,)), dma((Z,)), dma((Z,)), dma((C,)),
        ],
        compiler_params=pltpu.CompilerParams(
            collective_id=0, has_side_effects=True, vmem_limit_bytes=60 * 1024 * 1024
        ),
    )(acts, grads, frozen, ain, aout, mag)
    return pl.pallas_call(
        finish,
        out_shape=tuple(jax.ShapeDtypeStruct(x.shape, x.dtype) for x in (ig, ing, oug, mgrad)),
        in_specs=[vm] * 4,
        out_specs=(vm,) * 4,
    )(ig, ing, oug, mgrad)


def solution(mesh):
    return jax.shard_map(
        functools.partial(body, mesh.shape["row"], mesh.shape["col"]),
        mesh=mesh,
        in_specs=(
            P(None, "col", "row"),
            P(None, "row", "col"),
            P(None, "row", "col"),
            P(None, None, "row"),
            P(None, None, "col"),
            P(None, "col"),
        ),
        out_specs=(
            P(None, "col", "row"),
            P(None, None, "row"),
            P(None, None, "col"),
            P(None, "col"),
        ),
        check_vma=False,
    )
```

profile of v0, /device:TPU:0, one launch (start us, length us, event | category | flops | bytes accessed | tf_op | source)
XLA Modules:
  0.0 59.8 jit_solution(10132741241369352336)
XLA Ops:
  0.6 57.0 %shard_map.93 = (bf16[6,128,256]{2,1,0:T(8,128)(2,1)}, f32[6,32,256]{2,1,0:T(8,128)}, f32[6,32,512]{2,1,0:T(8,128)}, f32[6,512]{1,0:T(8,128)}) custom-call(bf16[6,128,256]{2,1,0:T(8,128)(2,1)} %acts_hbm.1, bf16[6,64,512]{2,1,0:T(8,128)(2,1)} %grads_hbm.1, bf16[6,256,512]{2,1,0:T(8,128)(2,1)} %frozen_hbm.1, bf16[6,32,256]{2,1,0:T(8,128)(2,1)} %ain_hbm.1, ...), custom_call_target="tpu_custom_call" | custom-call | tf_op jit(solution)/shard_map/pallas_call | solution.py:391
  57.7 2.2 %shard_map.94 = (bf16[6,128,256]{2,1,0:T(8,128)(2,1)}, f32[6,32,256]{2,1,0:T(8,128)}, f32[6,32,512]{2,1,0:T(8,128)}, f32[6,512]{1,0:T(8,128)}) custom-call(bf16[6,128,256]{2,1,0:T(8,128)(2,1)} %get-tuple-element.8.ig, f32[6,32,256]{2,1,0:T(8,128)} %get-tuple-element.9.ing, f32[6,32,512]{2,1,0:T(8,128)} %get-tuple-element.10.oug, ...), custom_call_target="tpu_custom_call" | custom-call | tf_op jit(solution)/shard_map/pallas_call | solution.py:420
where the time goes:
time: 60.5 us; the launch traced here: 59.8 us
  Pallas kernels  59.2 us (98%)
  between operations  0.64 us (1%)
    pallas_call x1, Pallas kernels, body(): pl.pallas_call(functools.partial(kernel, R, C), out_shape=(jax.ShapeDtype...  57 us
    pallas_call x1, Pallas kernels, body(): pl.pallas_call(finish, out_shape=tuple((jax.ShapeDtypeStruct(x.shape, x.d...  2.18 us

commit v1 on v0

--- a/solution.py
+++ b/solution.py
@@ -372,11 +372,13 @@
         copy.wait()
 
 
-def finish(ig, ing, oug, mgrad, ig_out, ing_out, oug_out, mgrad_out):
-    ig_out[...] = ig[...]
-    ing_out[...] = ing[...]
-    oug_out[...] = oug[...]
-    mgrad_out[...] = mgrad[...]
+def finish(ig, ing, oug, mgrad, ig_out, ing_out, oug_out, mgrad_out, sem):
+    pairs = ((ig, ig_out), (ing, ing_out), (oug, oug_out), (mgrad, mgrad_out))
+    copies = [pltpu.make_async_copy(a, b, sem.at[i]) for i, (a, b) in enumerate(pairs)]
+    for copy in copies:
+        copy.start()
+    for copy in copies:
+        copy.wait()
 
 
 def body(R, C, acts, grads, frozen, ain, aout, mag):
@@ -391,13 +393,13 @@
     ig, ing, oug, mgrad = pl.pallas_call(
         functools.partial(kernel, R, C),
         out_shape=(
-            jax.ShapeDtypeStruct((L, TC, KI), BF16),
-            jax.ShapeDtypeStruct((L, RANK, KI), F32),
-            jax.ShapeDtypeStruct((L, RANK, W), F32),
-            jax.ShapeDtypeStruct((L, W), F32),
+            V((L, TC, KI), BF16),
+            V((L, RANK, KI), F32),
+            V((L, RANK, W), F32),
+            V((L, W), F32),
         ),
         in_specs=[hbm] * 6,
-        out_specs=(hbm,) * 4,
+        out_specs=(vm,) * 4,
         scratch_shapes=[
             V(acts.shape, BF16), V(grads.shape, BF16), V(frozen.shape, BF16),
             V(ain.shape, BF16), V(aout.shape, BF16), V(mag.shape, F32),
@@ -421,7 +423,9 @@
         finish,
         out_shape=tuple(jax.ShapeDtypeStruct(x.shape, x.dtype) for x in (ig, ing, oug, mgrad)),
         in_specs=[vm] * 4,
-        out_specs=(vm,) * 4,
+        out_specs=(hbm,) * 4,
+        scratch_shapes=[dma((4,))],
+        compiler_params=pltpu.CompilerParams(vmem_limit_bytes=1024 * 1024),
     )(ig, ing, oug, mgrad)
 
 

time: 60.5 us -> 59.4 us (0.982)
  Pallas kernels: 59.2 us -> 58.2 us
    pallas_call x1, Pallas kernels: 2.18 us -> 0.98 us  [body(): pl.pallas_call(finish, out_shape=tuple((jax.ShapeDtypeStruct(x.shape, x.d...]
where the time goes in v1:
time: 59.4 us; the launch traced here: 58.8 us
  Pallas kernels  58.2 us (98%)
  between operations  0.64 us (1%)
    pallas_call x1, Pallas kernels, body(): pl.pallas_call(functools.partial(kernel, R, C), out_shape=(V((L, TC, KI),...  57.2 us

profile of v1, /device:TPU:0, one launch (start us, length us, event | category | flops | bytes accessed | tf_op | source)
XLA Modules:
  0.0 58.8 jit_solution(2443961733443408518)
XLA Ops:
  0.6 57.2 %shard_map.93 = (bf16[6,128,256]{2,1,0:T(8,128)(2,1)S(1)}, f32[6,32,256]{2,1,0:T(8,128)S(1)}, f32[6,32,512]{2,1,0:T(8,128)S(1)}, f32[6,512]{1,0:T(8,128)S(1)}) custom-call(bf16[6,128,256]{2,1,0:T(8,128)(2,1)} %acts_hbm.1, bf16[6,64,512]{2,1,0:T(8,128)(2,1)} %grads_hbm.1, bf16[6,256,512]{2,1,0:T(8,128)(2,1)} %frozen_hbm.1, bf16[6,32,256]{2,1,0:T(8,128)(2,1)} %ain_hbm.1, ...), custom_call_target="tpu_custom_call" | custom-call | tf_op jit(solution)/shard_map/pallas_call | solution.py:393
  57.8 1.0 %shard_map.94 = (bf16[6,128,256]{2,1,0:T(8,128)(2,1)}, f32[6,32,256]{2,1,0:T(8,128)}, f32[6,32,512]{2,1,0:T(8,128)}, f32[6,512]{1,0:T(8,128)}) custom-call(bf16[6,128,256]{2,1,0:T(8,128)(2,1)S(1)} %get-tuple-element.8.ig, f32[6,32,256]{2,1,0:T(8,128)S(1)} %get-tuple-element.9.ing, f32[6,32,512]{2,1,0:T(8,128)S(1)} %get-tuple-element.10.oug, ...), custom_call_target="tpu_custom_call" | custom-call | tf_op jit(solution)/shard_map/pallas_call | solution.py:422

commit v2 on v1

v2 whole, which is shorter than its diff:
```python
import functools

import jax
import jax.numpy as jnp
from jax import lax
from jax.experimental import pallas as pl
from jax.experimental.pallas import tpu as pltpu
from jax.sharding import PartitionSpec as P

MESH = pl.DeviceIdType.MESH
F32 = jnp.float32
BF16 = jnp.bfloat16


def mm(a, b, dims):
    return lax.dot_general(a, b, (dims, ((), ())), preferred_element_type=F32)


NAMES = (
    "acts", "grads", "frozen", "ain", "aout", "mag", "load", "G", "A", "merged", "ws", "asc", "sqm", "sq_sib",
    "sq_z", "sq_tot", "norms", "scl", "cor", "mag3", "mg3", "prod_buf", "qs", "q_sib", "q_all", "Qg", "Qc", "ims",
    "im_sib", "im_all", "im_fin", "dt", "q", "q_recv", "q1_r", "q2_s", "q2_r", "own", "hold", "rs1_s", "rs1_r",
    "rs2_s", "rs2_r", "send", "g_in", "g_fw", "a_in", "rs1_in", "rs2_in", "sq_in", "dt_in", "root_in", "out_in",
    "col_in", "sib_in", "q_in", "q1_in", "q2_in",
)


def scratch(R, C, L, TR, W, TC, KI, RANK):
    Z, T, H, KH = R // 2, TR * R, L // 2, KI // 2
    V, dma = pltpu.VMEM, pltpu.SemaphoreType.DMA
    wide = (2, L, 2, TC, KH) if C == 4 else (C, L, TC, KI)
    slim = (2, L, TC, KH) if C == 4 else (1, 1, 8, 128)
    col = (L, 4) if C == 4 else (L, C)
    pair = (L, 2, RANK, KH) if C == 4 else (L, 1, RANK, KI)
    return dict(
        acts=V((L, TC, KI), BF16), grads=V((L, TR, W), BF16), frozen=V((L, KI, W), BF16),
        ain=V((L, RANK, KI), BF16), aout=V((L, RANK, W), BF16), mag=V((L, W), F32), load=dma((6,)),
        G=V((L, T, W), BF16), A=V((L, T, KI), BF16), merged=V((L, KI, W), F32), ws=V((L, KI, W), BF16),
        asc=V((L, RANK, W), BF16),
        sqm=V((L, 1, W), F32), sq_sib=V((H, 1, W), F32), sq_z=V((Z, H, 1, W), F32), sq_tot=V((2, H, 1, W), F32),
        norms=V((L, 1, W), F32), scl=V((L, 1, W), F32), cor=V((L, 1, W), F32), mag3=V((L, 1, W), F32),
        mg3=V((L, 1, W), F32),
        prod_buf=V((T, KI), F32), qs=V((2, H, RANK, TC), F32), q_sib=V((H, RANK, TC), F32), q_all=V((Z, H, RANK, TC), F32),
        Qg=V((2, C, H, RANK, TC), BF16), Qc=V((L, RANK, T), BF16),
        ims=V((2, H, RANK, W), F32), im_sib=V((H, RANK, W), F32), im_all=V((Z, H, RANK, W), BF16),
        im_fin=V((2, H, RANK, W), BF16),
        dt=V((R, L, 1, W), F32), q=V(pair, BF16), q_recv=V((C,) + pair, BF16),
        q1_r=V(pair, BF16), q2_s=V(pair, BF16), q2_r=V(pair, BF16),
        own=V((L, TC, KI), F32), hold=V(slim, F32), rs1_s=V(wide, BF16), rs1_r=V(wide, BF16),
        rs2_s=V(slim, BF16), rs2_r=V(slim, BF16),
        send=dma((16,)), g_in=dma((L, Z)), g_fw=dma((L, Z)), a_in=dma(col), rs1_in=dma(col), rs2_in=dma((L, 2)),
        sq_in=dma((Z,)), dt_in=dma((L, R)), root_in=dma((2, Z)), out_in=dma((2,)), col_in=dma((C,)),
        sib_in=dma((6,)), q_in=dma((L, C)), q1_in=dma((L, 2)), q2_in=dma((L, 2)),
    )


def kernel(R, C, *refs):
    acts_hbm, grads_hbm, frozen_hbm, ain_hbm, aout_hbm, mag_hbm, ig, ing, oug, mgrad = refs[:10]
    (acts, grads, frozen, ain, aout, mag, load, G, A, merged, ws, asc, sqm, sq_sib, sq_z, sq_tot, norms, scl, cor,
     mag3, mg3, prod_buf, qs, q_sib, q_all, Qg, Qc, ims, im_sib, im_all, im_fin, dt, q, q_recv, q1_r, q2_s, q2_r,
     own, hold, rs1_s, rs1_r, rs2_s, rs2_r, send, g_in, g_fw, a_in, rs1_in, rs2_in, sq_in, dt_in, root_in, out_in, col_in,
     sib_in, q_in, q1_in, q2_in) = refs[10:]
    pairs = ((grads_hbm, grads), (acts_hbm, acts), (frozen_hbm, frozen),
             (ain_hbm, ain), (aout_hbm, aout), (mag_hbm, mag))
    loads = [pltpu.make_async_copy(a, b, load.at[i]) for i, (a, b) in enumerate(pairs)]
    for copy in loads:
        copy.start()
    L, TR, W = grads.shape
    TC, KI = acts.shape[1:]
    Z, H, KH = R // 2, L // 2, KI // 2
    ahead = min(3, L)
    last = L + Z - 3
    r, c = lax.axis_index("row"), lax.axis_index("col")
    z, core = r // 2, lax.rem(r, 2)
    sib = 2 * z + 1 - core
    square = C == 4
    xn, yn = c + 1 - 2 * lax.rem(c, 2), lax.rem(c + 2, 4)
    dg = 3 - c
    root = Z // 2 - 1 + core
    middle = jnp.logical_and(z > 0, z < Z - 1)
    halves = 2 if square else 1
    KS = KI // halves

    def row_to(d):
        return lax.rem(r + d, R)

    def row_from(d):
        return lax.rem(r + R - d, R)

    def col_to(d):
        return lax.rem(c + d, C)

    def col_from(d):
        return lax.rem(c + C - d, C)

    def z_to(d):
        return 2 * lax.rem(z + d, Z) + core

    def z_from(d):
        return lax.rem(z + Z - d, Z)

    def rows(at, size):
        return pl.ds(pl.multiple_of(at * size, size), size)

    def rcopy(src, dst, cat, recv, **dev):
        return pltpu.make_async_remote_copy(
            src_ref=src, dst_ref=dst, send_sem=send.at[cat], recv_sem=recv,
            device_id=dev, device_id_type=MESH,
        )

    def arrived(ref, recv):
        rcopy(ref, ref, 0, recv, row=r).wait_recv()

    barrier = pltpu.get_barrier_semaphore()
    for d in range(1, R):
        pl.semaphore_signal(barrier, inc=1, device_id={"row": row_to(d)}, device_id_type=MESH)
    for d in range(1, C):
        pl.semaphore_signal(barrier, inc=1, device_id={"col": col_to(d)}, device_id_type=MESH)
    pl.semaphore_wait(barrier, R + C - 2)

    def g_block(l, at, which):
        return G.at[l, rows(2 * at + which, TR)]

    def g_own(l, step):
        if step == 0:
            return rcopy(grads.at[l], g_block(l, z, core), 1, g_fw.at[l, z], row=sib)
        return rcopy(grads.at[l], g_block(l, z, core), 0, g_in.at[l, z], row=r + 2 * step)

    def g_pass(l, at, step):
        block = g_block(l, at, core)
        if step == 0:
            return rcopy(block, block, 1, g_fw.at[l, at], row=sib)
        return rcopy(block, block, 0, g_in.at[l, at], row=r + 2 * step)

    def g_own_each(l, act):
        @pl.when(z < Z - 1)
        def _():
            act(g_own(l, 1))

        @pl.when(z > 0)
        def _():
            act(g_own(l, -1))

        act(g_own(l, 0))

    def g_relay(l, d, act, arrive):
        for step in (1, -1):
            at = z - step * d

            @pl.when(jnp.logical_and(at >= 0, at < Z))
            def _():
                if arrive:
                    arrived(g_block(l, at, core), g_in.at[l, at])

                @pl.when(jnp.logical_and(z + step >= 0, z + step < Z))
                def _():
                    act(g_pass(l, at, step))

                act(g_pass(l, at, 0))

    def a_copies(l):
        mine = A.at[l, rows(c, TC)]
        if square:
            return [rcopy(acts.at[l], mine, 2, a_in.at[l, 0], col=xn), rcopy(acts.at[l], mine, 2, a_in.at[l, 1], col=yn)]
        return [rcopy(acts.at[l], mine, 2, a_in.at[l, d], col=col_to(d)) for d in range(1, C)]

    def a_half(l, of, part):
        size = TC // 2
        return A.at[l, rows(2 * of + part, size)]

    def a_passes(l):
        first, second = a_half(l, xn, 0), a_half(l, yn, 1)
        return [rcopy(first, first, 3, a_in.at[l, 2], col=yn), rcopy(second, second, 3, a_in.at[l, 3], col=xn)]

    def a_relay(l):
        arrived(A.at[l, rows(xn, TC)], a_in.at[l, 0])
        arrived(A.at[l, rows(yn, TC)], a_in.at[l, 1])
        for copy in a_passes(l):
            copy.start()

    def a_ready(l):
        if square:
            arrived(a_half(l, dg, 0), a_in.at[l, 2])
            arrived(a_half(l, dg, 1), a_in.at[l, 3])
        else:
            for d in range(1, C):
                arrived(A.at[l, rows(col_from(d), TC)], a_in.at[l, d])

    def rs1_copies(l):
        if square:
            return [rcopy(rs1_s.at[i, l], rs1_r.at[i, l], 4, rs1_in.at[l, i], col=to) for i, to in enumerate((xn, yn))]
        return [rcopy(rs1_s.at[d, l], rs1_r.at[d, l], 4, rs1_in.at[l, d], col=col_to(d)) for d in range(1, C)]

    def rs2_copies(l):
        return [rcopy(rs2_s.at[i, l], rs2_r.at[i, l], 5, rs2_in.at[l, i], col=to) for i, to in enumerate((yn, xn))]

    def rs_first(l, prod):
        if square:
            for i, near in enumerate((xn, yn)):
                rs1_s[i, l, 0] = prod[rows(near, TC), cols(i)].astype(BF16)
                rs1_s[i, l, 1] = prod[rows(dg, TC), cols(i)].astype(BF16)
                hold[i, l] = prod[rows((yn, xn)[i], TC), cols(i)]
        else:
            for d in range(1, C):
                rs1_s[d, l] = prod[rows(col_to(d), TC)].astype(BF16)
        own[l] = prod[rows(c, TC)]
        for copy in rs1_copies(l):
            copy.start()

    def rs_second(l):
        if square:
            for i in range(2):
                arrived(rs1_r.at[i, l], rs1_in.at[l, i])
                rs2_s[i, l] = (hold[i, l] + rs1_r[i, l, 1].astype(F32)).astype(BF16)
            for copy in rs2_copies(l):
                copy.start()

    def rs_finish(l):
        if square:
            for i in range(2):
                arrived(rs2_r.at[i, l], rs2_in.at[l, i])
                total = own[l, :, cols(i)] + rs1_r[i, l, 0].astype(F32) + rs2_r[i, l].astype(F32)
                ig[l, :, cols(i)] = total.astype(BF16)
        else:
            total = own[l]
            for d in range(1, C):
                arrived(rs1_r.at[d, l], rs1_in.at[l, d])
                total = total + rs1_r[d, l].astype(F32)
            ig[l] = total.astype(BF16)

    def sq_copy(d):
        return rcopy(sq_z.at[z], sq_z.at[z], 6, sq_in.at[d], row=z_to(d))

    to_sib = [
        rcopy(sqm.at[pl.ds((1 - core) * H, H)], sq_sib, 7, sib_in.at[0], row=sib),
        rcopy(sq_tot.at[core], sq_tot.at[core], 7, sib_in.at[1], row=sib),
        rcopy(qs.at[1 - core], q_sib, 7, sib_in.at[2], row=sib),
        rcopy(ims.at[1 - core], im_sib, 7, sib_in.at[3], row=sib),
        rcopy(Qg.at[core], Qg.at[core], 7, sib_in.at[4], row=sib),
        rcopy(im_fin.at[core], im_fin.at[core], 7, sib_in.at[5], row=sib),
    ]

    def root_copies():
        return [rcopy(q_all.at[z], q_all.at[z], 8, root_in.at[0, z], row=2 * root + core),
                rcopy(im_all.at[z], im_all.at[z], 9, root_in.at[1, z], row=2 * root + core)]

    def out_ref(i):
        return Qg.at[core, c] if i == 0 else im_fin.at[core]

    def out_copies(i):
        ref = out_ref(i)
        return [rcopy(ref, ref, 10 + i, out_in.at[i], row=z_to(d)) for d in range(1, Z)]

    def gather_copies():
        mine = Qg.at[core, c]
        return [rcopy(mine, mine, 12, col_in.at[d], col=col_to(d)) for d in range(1, C)]

    def start(copy):
        copy.start()

    def to_root():
        arrived(q_sib, sib_in.at[2])
        arrived(im_sib, sib_in.at[3])
        q_all[z] = qs[core] + q_sib[...]
        im_all[z] = (ims[core] + im_sib[...]).astype(BF16)

        @pl.when(z != root)
        def _():
            for copy in root_copies():
                copy.start()

    def at_root():
        for d in range(1, Z):
            arrived(q_all.at[z_from(d)], root_in.at[0, z_from(d)])
            arrived(im_all.at[z_from(d)], root_in.at[1, z_from(d)])
        q_sum, im_sum = q_all[0], im_all[0].astype(F32)
        for s in range(1, Z):
            q_sum = q_sum + q_all[s]
            im_sum = im_sum + im_all[s].astype(F32)
        Qg[core, c] = q_sum.astype(BF16)
        im_fin[core] = im_sum.astype(BF16)
        for copy in out_copies(0) + gather_copies():
            copy.start()

    def q_arrived():
        arrived(out_ref(0), out_in.at[0])
        for copy in gather_copies():
            copy.start()

    def dt_copy(l, d):
        return rcopy(dt.at[r, l], dt.at[r, l], 13, dt_in.at[l, d], row=row_to(d))

    def q_copies(l):
        return [rcopy(q.at[l], q_recv.at[d, l], 14, q_in.at[l, d], col=col_to(d)) for d in range(1, C)]

    def q1_copies(l):
        return [rcopy(q.at[l, i], q1_r.at[l, i], 15, q1_in.at[l, i], col=to) for i, to in enumerate((xn, yn))]

    def q2_copies(l):
        return [rcopy(q2_s.at[l, i], q2_r.at[l, i], 15, q2_in.at[l, i], col=to) for i, to in enumerate((yn, xn))]

    def cols(i):
        return slice(i * KS, (i + 1) * KS)

    loads[0].wait()
    loads[1].wait()

    @pl.loop(0, ahead)
    def _(l):
        g_own_each(l, start)

    @pl.loop(0, L)
    def _(l):
        for copy in a_copies(l):
            copy.start()

    for copy in loads[2:]:
        copy.wait()

    @pl.loop(0, L)
    def _(l):
        m = frozen[l].astype(F32) + mm(ain[l], aout[l], ((0,), (0,)))
        merged[l] = m
        sqm[l] = jnp.sum(m * m, axis=0, keepdims=True)

    to_sib[0].start()

    @pl.loop(0, L)
    def _(l):
        G[l, rows(r, TR)] = grads[l]
        A[l, rows(c, TC)] = acts[l]
        half, at = l // H, lax.rem(l, H)
        ims[half, at] = mm(ain[l], merged[l].astype(BF16), ((1,), (0,)))
        qs[half, at] = mm(ain[l], acts[l], ((1,), (1,)))

    to_sib[2].start()
    to_sib[3].start()
    for l in range(L):
        mag3[l] = mag[l:l + 1]

    def squares_out():
        arrived(sq_sib, sib_in.at[0])
        sq_z[z] = sqm[pl.ds(core * H, H)] + sq_sib[...]
        for d in range(1, Z):
            sq_copy(d).start()

    def squares_sum():
        for d in range(1, Z):
            arrived(sq_z.at[z_from(d)], sq_in.at[d])
        total = sq_z[0]
        for s in range(1, Z):
            total = total + sq_z[s]
        sq_tot[core] = total
        to_sib[1].start()

    def scales():
        arrived(sq_tot.at[1 - core], sib_in.at[1])

        @pl.loop(0, L)
        def _(l):
            n = jnp.sqrt(sq_tot[l // H, lax.rem(l, H)] + 0.25)
            s = mag3[l] / n
            norms[l] = n
            scl[l] = s
            ws[l] = (merged[l] * s).astype(BF16)
            asc[l] = (aout[l].astype(F32) * s).astype(BF16)

    def compute(l):
        for at in range(Z):
            arrived(g_block(l, at, 1 - core), g_fw.at[l, at])
        a_ready(l)
        g = G[l]
        outer = mm(A[l], g, ((0,), (0,)))
        dt[r, l] = jnp.sum(merged[l] * outer, axis=0, keepdims=True)
        for d in range(1, R):
            dt_copy(l, d).start()
        low = outer.astype(BF16)
        prod_buf[...] = mm(g, ws[l], ((1,), (1,)))
        rs_first(l, prod_buf)
        ing[l] = mm(asc[l], low, ((1,), (1,)))

        @pl.when(l > 1)
        def _():
            rs_second(l - 2)

    def correct(l, direct):
        for d in range(1, R):
            arrived(dt.at[row_from(d), l], dt_in.at[l, d])
        dots = dt[0, l]
        for s in range(1, R):
            dots = dots + dt[s, l]
        n = norms[l]
        mg3[l] = dots / n
        factor = -mag3[l] * dots / (n * n * n)
        cor[l] = factor
        adjusted = (merged[l] * factor).astype(BF16)
        part = ing[l] + mm(aout[l], adjusted, ((1,), (1,)))
        ing[l] = part
        for i in range(halves):
            q[l, i] = part[:, cols(i)].astype(BF16)
        for copy in q_copies(l) if direct else q1_copies(l):
            copy.start()

    def q_second(l):
        for i in range(2):
            arrived(q1_r.at[l, i], q1_in.at[l, i])
            total = ing[l, :, cols(i)] + q1_r[l, i].astype(F32)
            ing[l, :, cols(i)] = total
            q2_s[l, i] = total.astype(BF16)
        for copy in q2_copies(l):
            copy.start()

    def relays(at):
        @pl.when(at + ahead < L)
        def _():
            g_own_each(at + ahead, start)

        for d in range(1, Z):
            l = at - (d - 1)

            @pl.when(jnp.logical_and(l >= 0, l < L))
            def _():
                g_relay(l, d, start, True)

    squares_out()
    lead = 1

    @pl.when(middle)
    def _():
        for at in range(lead):
            relays(at)

    shift = jnp.where(middle, lead, 0)

    @pl.loop(0, last + 1)
    def _(at):
        relays(at + shift)

        if square:
            for l in (2 * at - 1, 2 * at):
                @pl.when(jnp.logical_and(l >= 0, l < L))
                def _():
                    a_relay(l)

        @pl.when(at == 1)
        def _():
            to_root()

        @pl.when(jnp.logical_and(at == min(last - 2, Z), z == root))
        def _():
            at_root()

        @pl.when(jnp.logical_and(at == last, z != root))
        def _():
            q_arrived()

        @pl.when(jnp.logical_and(at == last - 1, z == root))
        def _():
            for copy in out_copies(1):
                copy.start()
            to_sib[5].start()

        @pl.when(at == Z - 2)
        def _():
            squares_sum()
            scales()

        @pl.when(at >= Z - 2)
        def _():
            compute(at - (Z - 2))

        if square:
            @pl.when(jnp.logical_and(jnp.logical_not(middle), at - Z - 1 >= 0))
            def _():
                correct(at - Z - 1, False)

    rs_second(L - 2)

    @pl.loop(jnp.where(middle, 0, jnp.maximum(last - Z, 0)) if square else 0, L - 2)
    def _(l):
        correct(l, not square)

    for d in range(1, C):
        arrived(Qg.at[core, col_from(d)], col_in.at[d])
    to_sib[4].start()

    @pl.when(z != root)
    def _():
        arrived(out_ref(1), out_in.at[1])
        to_sib[5].start()

    correct(L - 2, not square)

    arrived(Qg.at[1 - core], sib_in.at[4])

    @pl.loop(0, L)
    def _(l):
        half, at = l // H, lax.rem(l, H)
        for s in range(C):
            Qc[l, :, s * TC:(s + 1) * TC] = Qg[half, s, at]
        oug[l] = mm(Qc[l], G[l], ((1,), (0,))) * scl[l]

    rs_second(L - 1)

    if square:
        @pl.loop(0, L - 1)
        def _(l):
            q_second(l)

    correct(L - 1, True)
    for l in range(L):
        mgrad[l:l + 1] = mg3[l]

    arrived(im_fin.at[1 - core], sib_in.at[5])

    @pl.loop(0, L)
    def _(l):
        oug[l] += im_fin[l // H, lax.rem(l, H)].astype(F32) * cor[l]

    @pl.loop(0, L)
    def _(l):
        rs_finish(l)

    if square:
        @pl.loop(0, L - 1)
        def _(l):
            for i in range(2):
                arrived(q2_r.at[l, i], q2_in.at[l, i])
                ing[l, :, cols(i)] += q2_r[l, i].astype(F32)

    @pl.loop(L - 1 if square else 0, L)
    def _(l):
        for i in range(halves):
            total = ing[l, :, cols(i)]
            for d in range(1, C):
                if i == 0:
                    arrived(q_recv.at[d, l], q_in.at[l, d])
                total = total + q_recv[d, l, i].astype(F32)
            ing[l, :, cols(i)] = total

    def done(copy):
        copy.wait_send()

    @pl.loop(0, L)
    def _(l):
        g_own_each(l, done)
        for d in range(1, Z):
            g_relay(l, d, done, False)
        sent = a_copies(l) + rs1_copies(l) + [dt_copy(l, d) for d in range(1, R)]
        if square:
            sent += a_passes(l) + rs2_copies(l)
        for copy in sent:
            copy.wait_send()

    @pl.loop(0, L - 1)
    def _(l):
        for copy in q1_copies(l) + q2_copies(l) if square else q_copies(l):
            copy.wait_send()

    for copy in to_sib + [sq_copy(d) for d in range(1, Z)] + gather_copies() + q_copies(L - 1):
        copy.wait_send()

    @pl.when(z == root)
    def _():
        for copy in out_copies(0) + out_copies(1):
            copy.wait_send()

    @pl.when(z != root)
    def _():
        for copy in root_copies():
            copy.wait_send()


def finish(ig, ing, oug, mgrad, ig_out, ing_out, oug_out, mgrad_out, sem):
    pairs = ((ig, ig_out), (ing, ing_out), (oug, oug_out), (mgrad, mgrad_out))
    copies = [pltpu.make_async_copy(a, b, sem.at[i]) for i, (a, b) in enumerate(pairs)]
    for copy in copies:
        copy.start()
    for copy in copies:
        copy.wait()


def body(R, C, acts, grads, frozen, ain, aout, mag):
    L, TR, W = grads.shape
    TC, KI = acts.shape[1:]
    RANK = ain.shape[1]
    V = pltpu.VMEM
    vm = pl.BlockSpec(memory_space=pltpu.VMEM)
    hbm = pl.BlockSpec(memory_space=pltpu.HBM)
    buffers = scratch(R, C, L, TR, W, TC, KI, RANK)
    ig, ing, oug, mgrad = pl.pallas_call(
        functools.partial(kernel, R, C),
        out_shape=(V((L, TC, KI), BF16), V((L, RANK, KI), F32), V((L, RANK, W), F32), V((L, W), F32)),
        in_specs=[hbm] * 6,
        out_specs=(vm,) * 4,
        scratch_shapes=[buffers[name] for name in NAMES],
        compiler_params=pltpu.CompilerParams(
            collective_id=0, has_side_effects=True, vmem_limit_bytes=60 * 1024 * 1024
        ),
    )(acts, grads, frozen, ain, aout, mag)
    return pl.pallas_call(
        finish,
        out_shape=tuple(jax.ShapeDtypeStruct(x.shape, x.dtype) for x in (ig, ing, oug, mgrad)),
        in_specs=[vm] * 4,
        out_specs=(hbm,) * 4,
        scratch_shapes=[pltpu.SemaphoreType.DMA((4,))],
        compiler_params=pltpu.CompilerParams(vmem_limit_bytes=1024 * 1024),
    )(ig, ing, oug, mgrad)


def solution(mesh):
    return jax.shard_map(
        functools.partial(body, mesh.shape["row"], mesh.shape["col"]),
        mesh=mesh,
        in_specs=(
            P(None, "col", "row"),
            P(None, "row", "col"),
            P(None, "row", "col"),
            P(None, None, "row"),
            P(None, None, "col"),
            P(None, "col"),
        ),
        out_specs=(
            P(None, "col", "row"),
            P(None, None, "row"),
            P(None, None, "col"),
            P(None, "col"),
        ),
        check_vma=False,
    )
```

time: 59.4 us -> 51.4 us (0.87)
  Pallas kernels: 58.2 us -> 50.6 us
    pallas_call x1, Pallas kernels: 57.2 us -> 49.6 us  [body(): pl.pallas_call(functools.partial(kernel, R, C), out_shape=(V((L, TC, KI),...]
where the time goes in v2:
time: 51.4 us; the launch traced here: 51.2 us
  Pallas kernels  50.6 us (98%)
  between operations  0.64 us (1%)
    pallas_call x1, Pallas kernels, body(): pl.pallas_call(functools.partial(kernel, R, C), out_shape=(V((L, TC, KI),...  49.6 us

profile of v2, /device:TPU:0, one launch (start us, length us, event | category | flops | bytes accessed | tf_op | source)
XLA Modules:
  0.0 51.2 jit_solution(16652648615762593519)
XLA Ops:
  0.6 49.6 %shard_map.93 = (bf16[6,128,256]{2,1,0:T(8,128)(2,1)S(1)}, f32[6,32,256]{2,1,0:T(8,128)S(1)}, f32[6,32,512]{2,1,0:T(8,128)S(1)}, f32[6,512]{1,0:T(8,128)S(1)}) custom-call(bf16[6,128,256]{2,1,0:T(8,128)(2,1)} %refs_0_.1, bf16[6,64,512]{2,1,0:T(8,128)(2,1)} %refs_1_.1, bf16[6,256,512]{2,1,0:T(8,128)(2,1)} %refs_2_.1, bf16[6,32,256]{2,1,0:T(8,128)(2,1)} %refs_3_.1, ...), custom_call_target="tpu_custom_call" | custom-call | tf_op jit(solution)/shard_map/pallas_call | solution.py:591
  50.2 1.0 %shard_map.94 = (bf16[6,128,256]{2,1,0:T(8,128)(2,1)}, f32[6,32,256]{2,1,0:T(8,128)}, f32[6,32,512]{2,1,0:T(8,128)}, f32[6,512]{1,0:T(8,128)}) custom-call(bf16[6,128,256]{2,1,0:T(8,128)(2,1)S(1)} %get-tuple-element.8.ig, f32[6,32,256]{2,1,0:T(8,128)S(1)} %get-tuple-element.9.ing, f32[6,32,512]{2,1,0:T(8,128)S(1)} %get-tuple-element.10.oug, ...), custom_call_target="tpu_custom_call" | custom-call | tf_op jit(solution)/shard_map/pallas_call | solution.py:601

commit v3 on v2

v3 whole, which is shorter than its diff:
```python
import functools

import jax
import jax.numpy as jnp
from jax import lax
from jax.experimental import pallas as pl
from jax.experimental.pallas import tpu as pltpu
from jax.sharding import PartitionSpec as P

MESH = pl.DeviceIdType.MESH
F32 = jnp.float32
BF16 = jnp.bfloat16


def mm(a, b, dims):
    return lax.dot_general(a, b, (dims, ((), ())), preferred_element_type=F32)


NAMES = (
    "acts", "grads", "frozen", "ain", "aout", "mag", "load", "G", "A", "merged", "ws", "asc", "sqm", "sq_sib", "sq_z",
    "sq_tot", "norms", "scl", "cor", "mag3", "mg3", "prod_buf", "qs", "q_sib", "q_all", "Qg", "Qc", "ims", "im_sib",
    "im_all", "im_fin", "dt_part", "dt_sib", "dt_z", "dt_tot", "dt_all", "q", "q_recv", "q1_r", "q2_s", "q2_r", "own",
    "hold", "rs1_s", "rs1_r", "rs2_s", "rs2_r", "send", "g_in", "g_fw", "a_in", "rs1_in", "rs2_in", "sq_in", "dt_in",
    "dt_last", "root_in", "out_in", "col_in", "sib_in", "news", "q_in", "q1_in", "q2_in",
)


def scratch(R, C, L, TR, W, TC, KI, RANK):
    Z, T, H, KH = R // 2, TR * R, L // 2, KI // 2
    V, dma = pltpu.VMEM, pltpu.SemaphoreType.DMA
    wide = (2, L, 2, TC, KH) if C == 4 else (C, L, TC, KI)
    slim = (2, L, TC, KH) if C == 4 else (1, 1, 8, 128)
    pair = (L, 2, RANK, KH) if C == 4 else (L, 1, RANK, KI)
    return dict(
        acts=V((L, TC, KI), BF16), grads=V((L, TR, W), BF16), frozen=V((L, KI, W), BF16),
        ain=V((L, RANK, KI), BF16), aout=V((L, RANK, W), BF16), mag=V((L, W), F32), load=dma((6,)),
        G=V((L, T, W), BF16), A=V((L, T, KI), BF16), merged=V((L, KI, W), F32), ws=V((L, KI, W), BF16),
        asc=V((L, RANK, W), BF16),
        sqm=V((L, 1, W), F32), sq_sib=V((H, 1, W), F32), sq_z=V((Z, H, 1, W), F32), sq_tot=V((2, H, 1, W), F32),
        norms=V((L, 1, W), F32), scl=V((L, 1, W), F32), cor=V((L, 1, W), F32), mag3=V((L, 1, W), F32),
        mg3=V((L, 1, W), F32),
        prod_buf=V((T, KI), F32), qs=V((2, H, RANK, TC), F32), q_sib=V((H, RANK, TC), F32), q_all=V((Z, H, RANK, TC), F32),
        Qg=V((2, C, H, RANK, TC), BF16), Qc=V((L, RANK, T), BF16),
        ims=V((2, H, RANK, W), F32), im_sib=V((H, RANK, W), F32), im_all=V((Z, H, RANK, W), BF16),
        im_fin=V((2, H, RANK, W), BF16),
        dt_part=V((L, 1, W), F32), dt_sib=V((L, 1, W), F32), dt_z=V((L, Z, 1, W), F32),
        dt_tot=V((L, 1, W), F32), dt_all=V((2, R, 1, W), F32), q=V(pair, BF16), q_recv=V((C,) + pair, BF16),
        q1_r=V(pair, BF16), q2_s=V(pair, BF16), q2_r=V(pair, BF16),
        own=V((L, TC, KI), F32), hold=V(slim, F32), rs1_s=V(wide, BF16), rs1_r=V(wide, BF16),
        rs2_s=V(slim, BF16), rs2_r=V(slim, BF16),
        send=dma((1,)), g_in=dma((L, Z - 1)), g_fw=dma((L,)), a_in=dma((L, 2)), rs1_in=dma((L,)), rs2_in=dma((1,)),
        sq_in=dma((1,)), dt_in=dma((3, L - 2)), dt_last=dma((2,)), root_in=dma((2,)), out_in=dma((2,)), col_in=dma((1,)),
        sib_in=dma((6,)), news=pltpu.SemaphoreType.REGULAR((2, max(Z - 2, 1))), q_in=dma((1,) if C == 4 else (L,)), q1_in=dma((L - 1,)), q2_in=dma((1,)),
    )


def kernel(R, C, *refs):
    acts_hbm, grads_hbm, frozen_hbm, ain_hbm, aout_hbm, mag_hbm, ig, ing, oug, mgrad = refs[:10]
    (acts, grads, frozen, ain, aout, mag, load, G, A, merged, ws, asc, sqm, sq_sib, sq_z, sq_tot, norms, scl, cor,
     mag3, mg3, prod_buf, qs, q_sib, q_all, Qg, Qc, ims, im_sib, im_all, im_fin, dt_part, dt_sib, dt_z, dt_tot,
     dt_all, q, q_recv, q1_r, q2_s, q2_r, own, hold, rs1_s, rs1_r, rs2_s, rs2_r, send, g_in, g_fw, a_in, rs1_in,
     rs2_in, sq_in, dt_in, dt_last, root_in, out_in, col_in, sib_in, news, q_in, q1_in, q2_in) = refs[10:]
    pairs = ((grads_hbm, grads), (acts_hbm, acts), (frozen_hbm, frozen),
             (ain_hbm, ain), (aout_hbm, aout), (mag_hbm, mag))
    loads = [pltpu.make_async_copy(a, b, load.at[i]) for i, (a, b) in enumerate(pairs)]
    for copy in loads:
        copy.start()
    L, TR, W = grads.shape
    TC, KI = acts.shape[1:]
    Z, H, KH = R // 2, L // 2, KI // 2
    ahead = min(3, L)
    last = L + Z - 3
    r, c = lax.axis_index("row"), lax.axis_index("col")
    z, core = r // 2, lax.rem(r, 2)
    sib = 2 * z + 1 - core
    square = C == 4
    xn, yn = c + 1 - 2 * lax.rem(c, 2), lax.rem(c + 2, 4)
    dg = 3 - c
    root = Z // 2 - 1 + core
    middle = jnp.logical_and(z > 0, z < Z - 1)
    halves = 2 if square else 1
    KS = KI // halves

    def row_to(d):
        return lax.rem(r + d, R)

    def row_from(d):
        return lax.rem(r + R - d, R)

    def col_to(d):
        return lax.rem(c + d, C)

    def col_from(d):
        return lax.rem(c + C - d, C)

    def z_to(d):
        return 2 * lax.rem(z + d, Z) + core

    def z_from(d):
        return lax.rem(z + Z - d, Z)

    def rows(at, size):
        return pl.ds(pl.multiple_of(at * size, size), size)

    def rcopy(src, dst, recv, **dev):
        return pltpu.make_async_remote_copy(
            src_ref=src, dst_ref=dst, send_sem=send.at[0], recv_sem=recv,
            device_id=dev, device_id_type=MESH,
        )

    def arrived(ref, recv):
        rcopy(ref, ref, recv, row=r).wait_recv()

    barrier = pltpu.get_barrier_semaphore()

    def greet(**dev):
        pl.semaphore_signal(barrier, inc=1, device_id=dev, device_id_type=MESH)

    greet(row=sib)
    for step in (1, -1):
        @pl.when(jnp.logical_and(z + step >= 0, z + step < Z))
        def _():
            greet(row=r + 2 * step)

    near = [xn, yn] if square else [col_to(d) for d in range(1, C)]
    for to in near:
        greet(col=to)
    pl.semaphore_wait(barrier, len(near) + jnp.where(middle, 3, 2))

    def tell(hops):
        for i, step in enumerate((1, -1)):
            of = z - step * (hops - 1)

            @pl.when((z + step >= 0) & (z + step < Z) & (of >= 0) & (of < Z))
            def _():
                pl.semaphore_signal(
                    news.at[i, hops - 2], inc=1, device_id={"row": r + 2 * step}, device_id_type=MESH
                )

    def hear(hops):
        for i, step in enumerate((1, -1)):
            of = z - step * hops

            @pl.when((of >= 0) & (of < Z))
            def _():
                pl.semaphore_wait(news.at[i, hops - 2], 1)

    def g_block(l, at, which):
        return G.at[l, rows(2 * at + which, TR)]

    def g_sem(l, at, to):
        return g_in.at[l, at - jnp.where(at > to, 1, 0)]

    def g_own(l, step):
        if step == 0:
            return rcopy(grads.at[l], g_block(l, z, core), g_fw.at[l], row=sib)
        return rcopy(grads.at[l], g_block(l, z, core), g_sem(l, z, z + step), row=r + 2 * step)

    def g_pass(l, at, step):
        block = g_block(l, at, core)
        if step == 0:
            return rcopy(block, block, g_fw.at[l], row=sib)
        return rcopy(block, block, g_sem(l, at, z + step), row=r + 2 * step)

    def g_own_each(l, act):
        @pl.when(z < Z - 1)
        def _():
            act(g_own(l, 1))

        @pl.when(z > 0)
        def _():
            act(g_own(l, -1))

        act(g_own(l, 0))

    def g_relay(l, d, act, arrive):
        for step in (1, -1):
            at = z - step * d

            @pl.when(jnp.logical_and(at >= 0, at < Z))
            def _():
                if arrive:
                    arrived(g_block(l, at, core), g_sem(l, at, z))

                @pl.when(jnp.logical_and(z + step >= 0, z + step < Z))
                def _():
                    act(g_pass(l, at, step))

                act(g_pass(l, at, 0))

    def a_copies(l):
        mine = A.at[l, rows(c, TC)]
        if square:
            return [rcopy(acts.at[l], mine, a_in.at[l, 0], col=xn), rcopy(acts.at[l], mine, a_in.at[l, 0], col=yn)]
        return [rcopy(acts.at[l], mine, a_in.at[l, 0], col=col_to(d)) for d in range(1, C)]

    def a_half(l, of, part):
        size = TC // 2
        return A.at[l, rows(2 * of + part, size)]

    def a_passes(l):
        first, second = a_half(l, xn, 0), a_half(l, yn, 1)
        return [rcopy(first, first, a_in.at[l, 1], col=yn), rcopy(second, second, a_in.at[l, 1], col=xn)]

    def a_relay(l):
        arrived(A.at[l, pl.ds(0, 2 * TC)], a_in.at[l, 0])
        for copy in a_passes(l):
            copy.start()

    def a_ready(l):
        if square:
            arrived(A.at[l, rows(dg, TC)], a_in.at[l, 1])
        else:
            arrived(A.at[l, pl.ds(0, (C - 1) * TC)], a_in.at[l, 0])

    def rs1_copies(l):
        if square:
            return [rcopy(rs1_s.at[i, l], rs1_r.at[i, l], rs1_in.at[l], col=to) for i, to in enumerate((xn, yn))]
        return [rcopy(rs1_s.at[d, l], rs1_r.at[d, l], rs1_in.at[l], col=col_to(d)) for d in range(1, C)]

    def rs2_copies(l):
        return [rcopy(rs2_s.at[i, l], rs2_r.at[i, l], rs2_in.at[0], col=to) for i, to in enumerate((yn, xn))]

    def rs_first(l, prod):
        if square:
            for i, near in enumerate((xn, yn)):
                rs1_s[i, l, 0] = prod[rows(near, TC), cols(i)].astype(BF16)
                rs1_s[i, l, 1] = prod[rows(dg, TC), cols(i)].astype(BF16)
                hold[i, l] = prod[rows((yn, xn)[i], TC), cols(i)]
        else:
            for d in range(1, C):
                rs1_s[d, l] = prod[rows(col_to(d), TC)].astype(BF16)
        own[l] = prod[rows(c, TC)]
        for copy in rs1_copies(l):
            copy.start()

    def rs_second(l):
        if square:
            arrived(rs1_r.at[:, l], rs1_in.at[l])
            for i in range(2):
                rs2_s[i, l] = (hold[i, l] + rs1_r[i, l, 1].astype(F32)).astype(BF16)
            for copy in rs2_copies(l):
                copy.start()

    def rs_finish(l):
        if square:
            for i in range(2):
                total = own[l, :, cols(i)] + rs1_r[i, l, 0].astype(F32) + rs2_r[i, l].astype(F32)
                ig[l, :, cols(i)] = total.astype(BF16)
        else:
            total = own[l]
            arrived(rs1_r.at[pl.ds(1, C - 1), l], rs1_in.at[l])
            for d in range(1, C):
                total = total + rs1_r[d, l].astype(F32)
            ig[l] = total.astype(BF16)

    def sq_copies():
        return [rcopy(sq_z.at[z], sq_z.at[z], sq_in.at[0], row=z_to(d)) for d in range(1, Z)]

    to_sib = [
        rcopy(sqm.at[pl.ds((1 - core) * H, H)], sq_sib, sib_in.at[0], row=sib),
        rcopy(sq_tot.at[core], sq_tot.at[core], sib_in.at[1], row=sib),
        rcopy(qs.at[1 - core], q_sib, sib_in.at[2], row=sib),
        rcopy(ims.at[1 - core], im_sib, sib_in.at[3], row=sib),
        rcopy(Qg.at[core], Qg.at[core], sib_in.at[4], row=sib),
        rcopy(im_fin.at[core], im_fin.at[core], sib_in.at[5], row=sib),
    ]

    def root_copies():
        return [rcopy(q_all.at[z], q_all.at[z], root_in.at[0], row=2 * root + core),
                rcopy(im_all.at[z], im_all.at[z], root_in.at[1], row=2 * root + core)]

    def out_ref(i):
        return Qg.at[core, c] if i == 0 else im_fin.at[core]

    def out_copies(i):
        ref = out_ref(i)
        return [rcopy(ref, ref, out_in.at[i], row=z_to(d)) for d in range(1, Z)]

    def gather_copies():
        mine = Qg.at[core, c]
        return [rcopy(mine, mine, col_in.at[0], col=col_to(d)) for d in range(1, C)]

    def start(copy):
        copy.start()

    def to_root():
        arrived(q_sib, sib_in.at[2])
        arrived(im_sib, sib_in.at[3])
        q_all[z] = qs[core] + q_sib[...]
        im_all[z] = (ims[core] + im_sib[...]).astype(BF16)

        @pl.when(z != root)
        def _():
            for copy in root_copies():
                copy.start()

    def at_root():
        arrived(q_all.at[pl.ds(0, Z - 1)], root_in.at[0])
        arrived(im_all.at[pl.ds(0, Z - 1)], root_in.at[1])
        q_sum, im_sum = q_all[0], im_all[0].astype(F32)
        for s in range(1, Z):
            q_sum = q_sum + q_all[s]
            im_sum = im_sum + im_all[s].astype(F32)
        Qg[core, c] = q_sum.astype(BF16)
        im_fin[core] = im_sum.astype(BF16)
        for copy in out_copies(0) + gather_copies():
            copy.start()

    def q_arrived():
        arrived(out_ref(0), out_in.at[0])
        for copy in gather_copies():
            copy.start()

    def dt_all_copies(l):
        mine = dt_all.at[l - (L - 2), r]
        return [rcopy(mine, mine, dt_last.at[l - (L - 2)], row=row_to(d)) for d in range(1, R)]

    def dt_sib_copy(l):
        return rcopy(dt_part.at[l], dt_sib.at[l], dt_in.at[0, l], row=sib)

    def dt_z_copies(l):
        return [rcopy(dt_z.at[l, z], dt_z.at[l, z], dt_in.at[1, l], row=z_to(d)) for d in range(1, Z)]

    def dt_tot_copy(l):
        return rcopy(dt_tot.at[l], dt_tot.at[l], dt_in.at[2, l], row=sib)

    def in_charge(l):
        return lax.rem(l, 2) == core

    def dots_out(l, part):
        @pl.when(l < L - 2)
        def _():
            dt_part[l] = part

            @pl.when(jnp.logical_not(in_charge(l)))
            def _():
                dt_sib_copy(l).start()

        @pl.when(l >= L - 2)
        def _():
            dt_all[l - (L - 2), r] = part
            for copy in dt_all_copies(l):
                copy.start()

    def dots_chip(l):
        @pl.when(in_charge(l))
        def _():
            arrived(dt_sib.at[l], dt_in.at[0, l])
            dt_z[l, z] = dt_part[l] + dt_sib[l]
            for copy in dt_z_copies(l):
                copy.start()

    def dots_sum(l):
        @pl.when(in_charge(l))
        def _():
            arrived(dt_z.at[l, pl.ds(0, Z - 1)], dt_in.at[1, l])
            total = dt_z[l, 0]
            for s in range(1, Z):
                total = total + dt_z[l, s]
            dt_tot[l] = total
            dt_tot_copy(l).start()

    def q_copies(l):
        return [rcopy(q.at[l], q_recv.at[d, l], q_in.at[0 if square else l], col=col_to(d)) for d in range(1, C)]

    def q1_copies(l):
        return [rcopy(q.at[l, i], q1_r.at[l, i], q1_in.at[l], col=to) for i, to in enumerate((xn, yn))]

    def q2_copies(l):
        return [rcopy(q2_s.at[l, i], q2_r.at[l, i], q2_in.at[0], col=to) for i, to in enumerate((yn, xn))]

    def cols(i):
        return slice(i * KS, (i + 1) * KS)

    loads[0].wait()
    loads[1].wait()

    @pl.loop(0, ahead)
    def _(l):
        g_own_each(l, start)

    @pl.loop(0, L)
    def _(l):
        for copy in a_copies(l):
            copy.start()

    if Z > 2:
        tell(2)
    for copy in loads[2:]:
        copy.wait()

    @pl.loop(0, L)
    def _(l):
        m = frozen[l].astype(F32) + mm(ain[l], aout[l], ((0,), (0,)))
        merged[l] = m
        sqm[l] = jnp.sum(m * m, axis=0, keepdims=True)

    to_sib[0].start()
    for hops in range(2, Z):
        hear(hops)
        if hops < Z - 1:
            tell(hops + 1)

    @pl.loop(0, L)
    def _(l):
        G[l, rows(r, TR)] = grads[l]
        A[l, rows(c, TC)] = acts[l]
        half, at = l // H, lax.rem(l, H)
        ims[half, at] = mm(ain[l], merged[l].astype(BF16), ((1,), (0,)))
        qs[half, at] = mm(ain[l], acts[l], ((1,), (1,)))

    to_sib[2].start()
    to_sib[3].start()
    for l in range(L):
        mag3[l] = mag[l:l + 1]

    def squares_out():
        arrived(sq_sib, sib_in.at[0])
        sq_z[z] = sqm[pl.ds(core * H, H)] + sq_sib[...]
        for copy in sq_copies():
            copy.start()

    def squares_sum():
        arrived(sq_z.at[pl.ds(0, Z - 1)], sq_in.at[0])
        total = sq_z[0]
        for s in range(1, Z):
            total = total + sq_z[s]
        sq_tot[core] = total
        to_sib[1].start()

    def scales():
        arrived(sq_tot.at[1 - core], sib_in.at[1])

        @pl.loop(0, L)
        def _(l):
            n = jnp.sqrt(sq_tot[l // H, lax.rem(l, H)] + 0.25)
            s = mag3[l] / n
            norms[l] = n
            scl[l] = s
            ws[l] = (merged[l] * s).astype(BF16)
            asc[l] = (aout[l].astype(F32) * s).astype(BF16)

    def compute(l):
        @pl.when(jnp.logical_and(l >= 1, l < L - 1))
        def _():
            dots_chip(l - 1)

        arrived(G.at[l, pl.ds(0, Z * TR)], g_fw.at[l])
        a_ready(l)
        g = G[l]
        outer = mm(A[l], g, ((0,), (0,)))
        dots_out(l, jnp.sum(merged[l] * outer, axis=0, keepdims=True))
        low = outer.astype(BF16)
        prod_buf[...] = mm(g, ws[l], ((1,), (1,)))
        rs_first(l, prod_buf)
        ing[l] = mm(asc[l], low, ((1,), (1,)))

        @pl.when(l > 1)
        def _():
            rs_second(l - 2)

    def correct(l, direct):
        if isinstance(l, int) and l >= L - 2:
            every = dt_all.at[l - (L - 2)]
            arrived(every.at[pl.ds(0, R - 1)], dt_last.at[l - (L - 2)])
            dots = every[0]
            for s in range(1, R):
                dots = dots + every[s]
        else:
            @pl.when(jnp.logical_not(in_charge(l)))
            def _():
                arrived(dt_tot.at[l], dt_in.at[2, l])

            dots = dt_tot[l]
        n = norms[l]
        mg3[l] = dots / n
        factor = -mag3[l] * dots / (n * n * n)
        cor[l] = factor
        adjusted = (merged[l] * factor).astype(BF16)
        part = ing[l] + mm(aout[l], adjusted, ((1,), (1,)))
        ing[l] = part
        for i in range(halves):
            q[l, i] = part[:, cols(i)].astype(BF16)
        for copy in q_copies(l) if direct else q1_copies(l):
            copy.start()

    def q_second(l):
        arrived(q1_r.at[l], q1_in.at[l])
        for i in range(2):
            total = ing[l, :, cols(i)] + q1_r[l, i].astype(F32)
            ing[l, :, cols(i)] = total
            q2_s[l, i] = total.astype(BF16)
        for copy in q2_copies(l):
            copy.start()

    def relays(at):
        @pl.when(at + ahead < L)
        def _():
            g_own_each(at + ahead, start)

        for d in range(1, Z):
            l = at - (d - 1)

            @pl.when(jnp.logical_and(l >= 0, l < L))
            def _():
                g_relay(l, d, start, True)

    squares_out()
    lead = 1

    @pl.when(middle)
    def _():
        for at in range(lead):
            relays(at)

    @pl.loop(0, last + 1)
    def _(at):
        relays(at + jnp.where(middle, lead, at // last))

        @pl.when(jnp.logical_and(jnp.logical_not(middle), at == last - 1))
        def _():
            relays(last)

        if square:
            for l in (2 * at - 1, 2 * at):
                @pl.when(jnp.logical_and(l >= 0, l < L))
                def _():
                    a_relay(l)

        @pl.when(at == Z - 2)
        def _():
            to_root()

        @pl.when(jnp.logical_and(at == last - 2, z == root))
        def _():
            at_root()

        @pl.when(jnp.logical_and(at == last, z != root))
        def _():
            q_arrived()

        @pl.when(at == Z - 2)
        def _():
            squares_sum()
            scales()

        @pl.when(at >= Z - 2)
        def _():
            compute(at - (Z - 2))

        for lag, act in ((2, dots_sum), (3, lambda l: correct(l, not square))):
            @pl.when(jnp.logical_and(jnp.logical_not(middle), at - (Z - 2) - lag >= 0))
            def _():
                act(at - (Z - 2) - lag)

    @pl.when(z == root)
    def _():
        for copy in out_copies(1):
            copy.start()
        to_sib[5].start()

    @pl.loop(jnp.where(middle, 0, L - 2), L - 2)
    def _(l):
        dots_sum(l)

    @pl.loop(jnp.where(middle, 0, max(L - 3, 0)), L - 2)
    def _(l):
        correct(l, not square)

    correct(L - 2, not square)

    rs_second(L - 2)

    arrived(Qg.at[core, pl.ds(0, C - 1)], col_in.at[0])
    to_sib[4].start()

    correct(L - 1, True)

    rs_second(L - 1)

    if square:
        @pl.loop(0, L - 1)
        def _(l):
            q_second(l)

    @pl.when(z != root)
    def _():
        arrived(out_ref(1), out_in.at[1])
        to_sib[5].start()

    for l in range(L):
        mgrad[l:l + 1] = mg3[l]

    arrived(Qg.at[1 - core], sib_in.at[4])

    arrived(im_fin.at[1 - core], sib_in.at[5])

    @pl.loop(0, L)
    def _(l):
        half, at = l // H, lax.rem(l, H)
        for s in range(C):
            Qc[l, :, s * TC:(s + 1) * TC] = Qg[half, s, at]
        low = mm(Qc[l], G[l], ((1,), (0,))) * scl[l]
        oug[l] = low + im_fin[half, at].astype(F32) * cor[l]

    def done(copy):
        copy.wait_send()

    @pl.loop(0, L)
    def _(l):
        g_own_each(l, done)
        for d in range(1, Z):
            g_relay(l, d, done, False)
        for copy in a_copies(l) + rs1_copies(l):
            copy.wait_send()
        if square:
            for copy in a_passes(l):
                copy.wait_send()

    @pl.loop(0, L - 2)
    def _(l):
        @pl.when(in_charge(l))
        def _():
            for copy in dt_z_copies(l) + [dt_tot_copy(l)]:
                copy.wait_send()

        @pl.when(jnp.logical_not(in_charge(l)))
        def _():
            dt_sib_copy(l).wait_send()

    for copy in sq_copies() + to_sib + gather_copies() + dt_all_copies(L - 2) + dt_all_copies(L - 1):
        copy.wait_send()

    @pl.when(z == root)
    def _():
        for copy in out_copies(0) + out_copies(1):
            copy.wait_send()

    @pl.when(z != root)
    def _():
        for copy in root_copies():
            copy.wait_send()

    if square:
        arrived(rs2_r, rs2_in.at[0])

    @pl.loop(0, L)
    def _(l):
        rs_finish(l)

    arrived(q_recv.at[pl.ds(1, C - 1), L - 1], q_in.at[0 if square else L - 1])
    for i in range(halves):
        total = ing[L - 1, :, cols(i)]
        for d in range(1, C):
            total = total + q_recv[d, L - 1, i].astype(F32)
        ing[L - 1, :, cols(i)] = total

    if square:
        arrived(q2_r.at[pl.ds(0, L - 1)], q2_in.at[0])

    @pl.loop(0, L - 1)
    def _(l):
        if not square:
            arrived(q_recv.at[pl.ds(1, C - 1), l], q_in.at[0 if square else l])
        for i in range(halves):
            total = ing[l, :, cols(i)]
            if square:
                total = total + q2_r[l, i].astype(F32)
            else:
                for d in range(1, C):
                    total = total + q_recv[d, l, i].astype(F32)
            ing[l, :, cols(i)] = total

    @pl.loop(0, L)
    def _(l):
        if square:
            for copy in rs2_copies(l):
                copy.wait_send()

    @pl.loop(0, L - 1)
    def _(l):
        for copy in q1_copies(l) + q2_copies(l) if square else q_copies(l):
            copy.wait_send()

    for copy in q_copies(L - 1):
        copy.wait_send()


def finish(ig, ing, oug, mgrad, ig_out, ing_out, oug_out, mgrad_out, sem):
    pairs = ((ig, ig_out), (ing, ing_out), (oug, oug_out), (mgrad, mgrad_out))
    copies = [pltpu.make_async_copy(a, b, sem.at[i]) for i, (a, b) in enumerate(pairs)]
    for copy in copies:
        copy.start()
    for copy in copies:
        copy.wait()


def body(R, C, acts, grads, frozen, ain, aout, mag):
    L, TR, W = grads.shape
    TC, KI = acts.shape[1:]
    RANK = ain.shape[1]
    V = pltpu.VMEM
    vm = pl.BlockSpec(memory_space=pltpu.VMEM)
    hbm = pl.BlockSpec(memory_space=pltpu.HBM)
    buffers = scratch(R, C, L, TR, W, TC, KI, RANK)
    ig, ing, oug, mgrad = pl.pallas_call(
        functools.partial(kernel, R, C),
        out_shape=(V((L, TC, KI), BF16), V((L, RANK, KI), F32), V((L, RANK, W), F32), V((L, W), F32)),
        in_specs=[hbm] * 6,
        out_specs=(vm,) * 4,
        scratch_shapes=[buffers[name] for name in NAMES],
        compiler_params=pltpu.CompilerParams(
            collective_id=0, has_side_effects=True, vmem_limit_bytes=60 * 1024 * 1024
        ),
    )(acts, grads, frozen, ain, aout, mag)
    return pl.pallas_call(
        finish,
        out_shape=tuple(jax.ShapeDtypeStruct(x.shape, x.dtype) for x in (ig, ing, oug, mgrad)),
        in_specs=[vm] * 4,
        out_specs=(hbm,) * 4,
        scratch_shapes=[pltpu.SemaphoreType.DMA((4,))],
        compiler_params=pltpu.CompilerParams(vmem_limit_bytes=1024 * 1024),
    )(ig, ing, oug, mgrad)


def solution(mesh):
    return jax.shard_map(
        functools.partial(body, mesh.shape["row"], mesh.shape["col"]),
        mesh=mesh,
        in_specs=(
            P(None, "col", "row"),
            P(None, "row", "col"),
            P(None, "row", "col"),
            P(None, None, "row"),
            P(None, None, "col"),
            P(None, "col"),
        ),
        out_specs=(
            P(None, "col", "row"),
            P(None, None, "row"),
            P(None, None, "col"),
            P(None, "col"),
        ),
        check_vma=False,
    )
```

time: 51.4 us -> 47.4 us (0.922)
  Pallas kernels: 50.6 us -> 46.6 us
    pallas_call x1, Pallas kernels: 49.6 us -> 45.6 us  [body(): pl.pallas_call(functools.partial(kernel, R, C), out_shape=(V((L, TC, KI),...]
where the time goes in v3:
time: 47.4 us; the launch traced here: 47.2 us
  Pallas kernels  46.6 us (98%)
  between operations  0.64 us (1%)
    pallas_call x1, Pallas kernels, body(): pl.pallas_call(functools.partial(kernel, R, C), out_shape=(V((L, TC, KI),...  45.6 us
    pallas_call x1, Pallas kernels, body(): pl.pallas_call(finish, out_shape=tuple((jax.ShapeDtypeStruct(x.shape, x.d...  0.98 us

profile of v3, /device:TPU:0, one launch (start us, length us, event | category | flops | bytes accessed | tf_op | source)
XLA Modules:
  0.0 47.2 jit_solution(14167904739162904464)
XLA Ops:
  0.6 45.6 %shard_map.93 = (bf16[6,128,256]{2,1,0:T(8,128)(2,1)S(1)}, f32[6,32,256]{2,1,0:T(8,128)S(1)}, f32[6,32,512]{2,1,0:T(8,128)S(1)}, f32[6,512]{1,0:T(8,128)S(1)}) custom-call(bf16[6,128,256]{2,1,0:T(8,128)(2,1)} %refs_0_.1, bf16[6,64,512]{2,1,0:T(8,128)(2,1)} %refs_1_.1, bf16[6,256,512]{2,1,0:T(8,128)(2,1)} %refs_2_.1, bf16[6,32,256]{2,1,0:T(8,128)(2,1)} %refs_3_.1, ...), custom_call_target="tpu_custom_call" | custom-call | tf_op jit(solution)/shard_map/pallas_call | solution.py:707
  46.3 1.0 %shard_map.94 = (bf16[6,128,256]{2,1,0:T(8,128)(2,1)}, f32[6,32,256]{2,1,0:T(8,128)}, f32[6,32,512]{2,1,0:T(8,128)}, f32[6,512]{1,0:T(8,128)}) custom-call(bf16[6,128,256]{2,1,0:T(8,128)(2,1)S(1)} %get-tuple-element.8.ig, f32[6,32,256]{2,1,0:T(8,128)S(1)} %get-tuple-element.9.ing, f32[6,32,512]{2,1,0:T(8,128)S(1)} %get-tuple-element.10.oug, ...), custom_call_target="tpu_custom_call" | custom-call | tf_op jit(solution)/shard_map/pallas_call | solution.py:717

commit v4 on v3

--- a/solution.py
+++ b/solution.py
@@ -19,7 +19,7 @@
 NAMES = (
     "acts", "grads", "frozen", "ain", "aout", "mag", "load", "G", "A", "merged", "ws", "asc", "sqm", "sq_sib", "sq_z",
     "sq_tot", "norms", "scl", "cor", "mag3", "mg3", "prod_buf", "qs", "q_sib", "q_all", "Qg", "Qc", "ims", "im_sib",
-    "im_all", "im_fin", "dt_part", "dt_sib", "dt_z", "dt_tot", "dt_all", "q", "q_recv", "q1_r", "q2_s", "q2_r", "own",
+    "im_all", "im_fin", "dt_own", "dt_tot", "dt_all", "q", "q_recv", "q1_r", "q2_s", "q2_r", "own",
     "hold", "rs1_s", "rs1_r", "rs2_s", "rs2_r", "send", "g_in", "g_fw", "a_in", "rs1_in", "rs2_in", "sq_in", "dt_in",
     "dt_last", "root_in", "out_in", "col_in", "sib_in", "news", "q_in", "q1_in", "q2_in",
 )
@@ -43,21 +43,21 @@
         Qg=V((2, C, H, RANK, TC), BF16), Qc=V((L, RANK, T), BF16),
         ims=V((2, H, RANK, W), F32), im_sib=V((H, RANK, W), F32), im_all=V((Z, H, RANK, W), BF16),
         im_fin=V((2, H, RANK, W), BF16),
-        dt_part=V((L, 1, W), F32), dt_sib=V((L, 1, W), F32), dt_z=V((L, Z, 1, W), F32),
+        dt_own=V((L, R, 1, W), F32),
         dt_tot=V((L, 1, W), F32), dt_all=V((2, R, 1, W), F32), q=V(pair, BF16), q_recv=V((C,) + pair, BF16),
         q1_r=V(pair, BF16), q2_s=V(pair, BF16), q2_r=V(pair, BF16),
         own=V((L, TC, KI), F32), hold=V(slim, F32), rs1_s=V(wide, BF16), rs1_r=V(wide, BF16),
         rs2_s=V(slim, BF16), rs2_r=V(slim, BF16),
         send=dma((1,)), g_in=dma((L, Z - 1)), g_fw=dma((L,)), a_in=dma((L, 2)), rs1_in=dma((L,)), rs2_in=dma((1,)),
-        sq_in=dma((1,)), dt_in=dma((3, L - 2)), dt_last=dma((2,)), root_in=dma((2,)), out_in=dma((2,)), col_in=dma((1,)),
-        sib_in=dma((6,)), news=pltpu.SemaphoreType.REGULAR((2, max(Z - 2, 1))), q_in=dma((1,) if C == 4 else (L,)), q1_in=dma((L - 1,)), q2_in=dma((1,)),
+        sq_in=dma((1,)), dt_in=dma((2, L - 2)), dt_last=dma((2,)), root_in=dma((2,)), out_in=dma((2,)), col_in=dma((1,)),
+        sib_in=dma((6,)), news=pltpu.SemaphoreType.REGULAR((2, max(Z - 2, 1))), q_in=dma((L,)), q1_in=dma((L - 2,)), q2_in=dma((1,)),
     )
 
 
 def kernel(R, C, *refs):
     acts_hbm, grads_hbm, frozen_hbm, ain_hbm, aout_hbm, mag_hbm, ig, ing, oug, mgrad = refs[:10]
     (acts, grads, frozen, ain, aout, mag, load, G, A, merged, ws, asc, sqm, sq_sib, sq_z, sq_tot, norms, scl, cor,
-     mag3, mg3, prod_buf, qs, q_sib, q_all, Qg, Qc, ims, im_sib, im_all, im_fin, dt_part, dt_sib, dt_z, dt_tot,
+     mag3, mg3, prod_buf, qs, q_sib, q_all, Qg, Qc, ims, im_sib, im_all, im_fin, dt_own, dt_tot,
      dt_all, q, q_recv, q1_r, q2_s, q2_r, own, hold, rs1_s, rs1_r, rs2_s, rs2_r, send, g_in, g_fw, a_in, rs1_in,
      rs2_in, sq_in, dt_in, dt_last, root_in, out_in, col_in, sib_in, news, q_in, q1_in, q2_in) = refs[10:]
     pairs = ((grads_hbm, grads), (acts_hbm, acts), (frozen_hbm, frozen),
@@ -78,6 +78,7 @@
     dg = 3 - c
     root = Z // 2 - 1 + core
     middle = jnp.logical_and(z > 0, z < Z - 1)
+    ends = jnp.logical_not(middle)
     halves = 2 if square else 1
     KS = KI // halves
 
@@ -158,7 +159,7 @@
 
     def g_pass(l, at, step):
         block = g_block(l, at, core)
-        if step == 0:
+        if isinstance(step, int) and step == 0:
             return rcopy(block, block, g_fw.at[l], row=sib)
         return rcopy(block, block, g_sem(l, at, z + step), row=r + 2 * step)
 
@@ -173,20 +174,19 @@
 
         act(g_own(l, 0))
 
-    def g_relay(l, d, act, arrive):
-        for step in (1, -1):
-            at = z - step * d
-
-            @pl.when(jnp.logical_and(at >= 0, at < Z))
+    def g_relay(l, d, step, act, arrive):
+        at = z - step * d
+
+        @pl.when(jnp.logical_and(at >= 0, at < Z))
+        def _():
+            if arrive:
+                arrived(g_block(l, at, core), g_sem(l, at, z))
+
+            @pl.when(jnp.logical_and(z + step >= 0, z + step < Z))
             def _():
-                if arrive:
-                    arrived(g_block(l, at, core), g_sem(l, at, z))
-
-                @pl.when(jnp.logical_and(z + step >= 0, z + step < Z))
-                def _():
-                    act(g_pass(l, at, step))
-
-                act(g_pass(l, at, 0))
+                act(g_pass(l, at, step))
+
+            act(g_pass(l, at, 0))
 
     def a_copies(l):
         mine = A.at[l, rows(c, TC)]
@@ -316,14 +316,20 @@
         mine = dt_all.at[l - (L - 2), r]
         return [rcopy(mine, mine, dt_last.at[l - (L - 2)], row=row_to(d)) for d in range(1, R)]
 
-    def dt_sib_copy(l):
-        return rcopy(dt_part.at[l], dt_sib.at[l], dt_in.at[0, l], row=sib)
-
-    def dt_z_copies(l):
-        return [rcopy(dt_z.at[l, z], dt_z.at[l, z], dt_in.at[1, l], row=z_to(d)) for d in range(1, Z)]
+    def dt_own_copy(l, at):
+        mine = dt_own.at[l, r]
+        return rcopy(mine, mine, dt_in.at[0, l], row=2 * at + lax.rem(l, 2))
+
+    def dt_own_each(l, act):
+        for d in range(1, Z):
+            act(dt_own_copy(l, lax.rem(z + d, Z)))
+
+        @pl.when(jnp.logical_not(in_charge(l)))
+        def _():
+            act(dt_own_copy(l, z))
 
     def dt_tot_copy(l):
-        return rcopy(dt_tot.at[l], dt_tot.at[l], dt_in.at[2, l], row=sib)
+        return rcopy(dt_tot.at[l], dt_tot.at[l], dt_in.at[1, l], row=sib)
 
     def in_charge(l):
         return lax.rem(l, 2) == core
@@ -331,11 +337,8 @@
     def dots_out(l, part):
         @pl.when(l < L - 2)
         def _():
-            dt_part[l] = part
-
-            @pl.when(jnp.logical_not(in_charge(l)))
-            def _():
-                dt_sib_copy(l).start()
+            dt_own[l, r] = part
+            dt_own_each(l, start)
 
         @pl.when(l >= L - 2)
         def _():
@@ -343,26 +346,18 @@
             for copy in dt_all_copies(l):
                 copy.start()
 
-    def dots_chip(l):
-        @pl.when(in_charge(l))
-        def _():
-            arrived(dt_sib.at[l], dt_in.at[0, l])
-            dt_z[l, z] = dt_part[l] + dt_sib[l]
-            for copy in dt_z_copies(l):
-                copy.start()
-
     def dots_sum(l):
         @pl.when(in_charge(l))
         def _():
-            arrived(dt_z.at[l, pl.ds(0, Z - 1)], dt_in.at[1, l])
-            total = dt_z[l, 0]
-            for s in range(1, Z):
-                total = total + dt_z[l, s]
+            arrived(dt_own.at[l, pl.ds(0, R - 1)], dt_in.at[0, l])
+            total = dt_own[l, 0]
+            for s in range(1, R):
+                total = total + dt_own[l, s]
             dt_tot[l] = total
             dt_tot_copy(l).start()
 
     def q_copies(l):
-        return [rcopy(q.at[l], q_recv.at[d, l], q_in.at[0 if square else l], col=col_to(d)) for d in range(1, C)]
+        return [rcopy(q.at[l], q_recv.at[d, l], q_in.at[l], col=col_to(d)) for d in range(1, C)]
 
     def q1_copies(l):
         return [rcopy(q.at[l, i], q1_r.at[l, i], q1_in.at[l], col=to) for i, to in enumerate((xn, yn))]
@@ -441,24 +436,41 @@
             ws[l] = (merged[l] * s).astype(BF16)
             asc[l] = (aout[l].astype(F32) * s).astype(BF16)
 
+    out = jnp.where(z < Z // 2, -1, 1)
+
+    def relay(at, d, step):
+        l = at - (d - 1)
+
+        @pl.when(jnp.logical_and(l >= 0, l < L))
+        def _():
+            g_relay(l, d, step, start, True)
+
     def compute(l):
-        @pl.when(jnp.logical_and(l >= 1, l < L - 1))
-        def _():
-            dots_chip(l - 1)
+        back = jnp.where(middle, 3, 2)
+
+        @pl.when(l >= back)
+        def _():
+            rs_second(l - back)
 
         arrived(G.at[l, pl.ds(0, Z * TR)], g_fw.at[l])
         a_ready(l)
         g = G[l]
         outer = mm(A[l], g, ((0,), (0,)))
         dots_out(l, jnp.sum(merged[l] * outer, axis=0, keepdims=True))
+
+        @pl.when(jnp.logical_and(ends, l == L - 2))
+        def _():
+            relay(last - 1, Z - 2, out)
+
         low = outer.astype(BF16)
         prod_buf[...] = mm(g, ws[l], ((1,), (1,)))
         rs_first(l, prod_buf)
+
+        @pl.when(jnp.logical_and(ends, l == L - 2))
+        def _():
+            relay(last, Z - 1, out)
+
         ing[l] = mm(asc[l], low, ((1,), (1,)))
-
-        @pl.when(l > 1)
-        def _():
-            rs_second(l - 2)
 
     def correct(l, direct):
         if isinstance(l, int) and l >= L - 2:
@@ -470,7 +482,7 @@
         else:
             @pl.when(jnp.logical_not(in_charge(l)))
             def _():
-                arrived(dt_tot.at[l], dt_in.at[2, l])
+                arrived(dt_tot.at[l], dt_in.at[1, l])
 
             dots = dt_tot[l]
         n = norms[l]
@@ -494,17 +506,26 @@
         for copy in q2_copies(l):
             copy.start()
 
+    def own_at(at):
+        @pl.when(at + ahead < L)
+        def _():
+            g_own_each(at + ahead, start)
+
     def relays(at):
-        @pl.when(at + ahead < L)
-        def _():
-            g_own_each(at + ahead, start)
-
-        for d in range(1, Z):
-            l = at - (d - 1)
-
-            @pl.when(jnp.logical_and(l >= 0, l < L))
-            def _():
-                g_relay(l, d, start, True)
+        own_at(at)
+
+        @pl.when(at < Z - 2)
+        def _():
+            for d in range(1, Z):
+                relay(at, d, -out)
+                relay(at, d, out)
+
+        @pl.when(at >= Z - 2)
+        def _():
+            for d in range(1, Z):
+                relay(at, d, -out)
+            for d in range(Z - 1, 0, -1):
+                relay(at, d, out)
 
     squares_out()
     lead = 1
@@ -516,11 +537,16 @@
 
     @pl.loop(0, last + 1)
     def _(at):
-        relays(at + jnp.where(middle, lead, at // last))
-
-        @pl.when(jnp.logical_and(jnp.logical_not(middle), at == last - 1))
-        def _():
-            relays(last)
+        late = jnp.logical_and(jnp.logical_not(middle), at >= Z - 2)
+
+        @pl.when(jnp.logical_not(late))
+        def _():
+            relays(at + jnp.where(middle, lead, 0))
+
+        @pl.when(jnp.logical_and(late, at < last))
+        def _():
+            own_at(at)
+            relay(at, Z - 1, out)
 
         if square:
             for l in (2 * at - 1, 2 * at):
@@ -528,31 +554,50 @@
                 def _():
                     a_relay(l)
 
+        @pl.when(at == max(Z - 3, 0))
+        def _():
+            squares_sum()
+
         @pl.when(at == Z - 2)
         def _():
             to_root()
 
-        @pl.when(jnp.logical_and(at == last - 2, z == root))
+        @pl.when(jnp.logical_and(at == jnp.where(middle, last, last - 1), z != root))
+        def _():
+            q_arrived()
+
+        @pl.when(at == Z - 2)
+        def _():
+            scales()
+
+        @pl.when(at >= Z - 2)
+        def _():
+            compute(at - (Z - 2))
+
+        @pl.when(jnp.logical_and(late, at < last - 1))
+        def _():
+            for d in range(Z - 2, 0, -1):
+                relay(at, d, out)
+
+        @pl.when(jnp.logical_and(at == last - 4, z == root))
         def _():
             at_root()
 
-        @pl.when(jnp.logical_and(at == last, z != root))
-        def _():
-            q_arrived()
-
-        @pl.when(at == Z - 2)
-        def _():
-            squares_sum()
-            scales()
-
-        @pl.when(at >= Z - 2)
-        def _():
-            compute(at - (Z - 2))
-
-        for lag, act in ((2, dots_sum), (3, lambda l: correct(l, not square))):
-            @pl.when(jnp.logical_and(jnp.logical_not(middle), at - (Z - 2) - lag >= 0))
-            def _():
-                act(at - (Z - 2) - lag)
+        @pl.when(jnp.logical_and(ends, at >= last - 3))
+        def _():
+            dots_sum(at - (last - 3))
+
+        @pl.when(jnp.logical_and(ends, at == last - 2))
+        def _():
+            correct(0, not square)
+
+    @pl.loop(jnp.where(middle, 0, L - 2), L - 2)
+    def _(l):
+        dots_sum(l)
+
+    @pl.loop(jnp.where(middle, 0, 1), L - 3)
+    def _(l):
+        correct(l, not square)
 
     @pl.when(z == root)
     def _():
@@ -560,27 +605,34 @@
             copy.start()
         to_sib[5].start()
 
-    @pl.loop(jnp.where(middle, 0, L - 2), L - 2)
-    def _(l):
-        dots_sum(l)
-
-    @pl.loop(jnp.where(middle, 0, max(L - 3, 0)), L - 2)
-    def _(l):
-        correct(l, not square)
-
-    correct(L - 2, not square)
-
-    rs_second(L - 2)
-
     arrived(Qg.at[core, pl.ds(0, C - 1)], col_in.at[0])
     to_sib[4].start()
 
+    correct(L - 3, not square)
+
+    arrived(Qg.at[1 - core], sib_in.at[4])
+
+    @pl.loop(0, L)
+    def _(l):
+        half, at = l // H, lax.rem(l, H)
+        for s in range(C):
+            Qc[l, :, s * TC:(s + 1) * TC] = Qg[half, s, at]
+        oug[l] = mm(Qc[l], G[l], ((1,), (0,))) * scl[l]
+
+    @pl.when(middle)
+    def _():
+        rs_second(L - 3)
+
+    rs_second(L - 2)
+
+    correct(L - 2, True)
+
     correct(L - 1, True)
 
     rs_second(L - 1)
 
     if square:
-        @pl.loop(0, L - 1)
+        @pl.loop(0, L - 2)
         def _(l):
             q_second(l)
 
@@ -592,17 +644,11 @@
     for l in range(L):
         mgrad[l:l + 1] = mg3[l]
 
-    arrived(Qg.at[1 - core], sib_in.at[4])
-
     arrived(im_fin.at[1 - core], sib_in.at[5])
 
     @pl.loop(0, L)
     def _(l):
-        half, at = l // H, lax.rem(l, H)
-        for s in range(C):
-            Qc[l, :, s * TC:(s + 1) * TC] = Qg[half, s, at]
-        low = mm(Qc[l], G[l], ((1,), (0,))) * scl[l]
-        oug[l] = low + im_fin[half, at].astype(F32) * cor[l]
+        oug[l] += im_fin[l // H, lax.rem(l, H)].astype(F32) * cor[l]
 
     def done(copy):
         copy.wait_send()
@@ -611,8 +657,9 @@
     def _(l):
         g_own_each(l, done)
         for d in range(1, Z):
-            g_relay(l, d, done, False)
-        for copy in a_copies(l) + rs1_copies(l):
+            g_relay(l, d, 1, done, False)
+            g_relay(l, d, -1, done, False)
+        for copy in a_copies(l):
             copy.wait_send()
         if square:
             for copy in a_passes(l):
@@ -620,14 +667,11 @@
 
     @pl.loop(0, L - 2)
     def _(l):
+        dt_own_each(l, done)
+
         @pl.when(in_charge(l))
         def _():
-            for copy in dt_z_copies(l) + [dt_tot_copy(l)]:
-                copy.wait_send()
-
-        @pl.when(jnp.logical_not(in_charge(l)))
-        def _():
-            dt_sib_copy(l).wait_send()
+            dt_tot_copy(l).wait_send()
 
     for copy in sq_copies() + to_sib + gather_copies() + dt_all_copies(L - 2) + dt_all_copies(L - 1):
         copy.wait_send()
@@ -649,41 +693,34 @@
     def _(l):
         rs_finish(l)
 
-    arrived(q_recv.at[pl.ds(1, C - 1), L - 1], q_in.at[0 if square else L - 1])
-    for i in range(halves):
-        total = ing[L - 1, :, cols(i)]
-        for d in range(1, C):
-            total = total + q_recv[d, L - 1, i].astype(F32)
-        ing[L - 1, :, cols(i)] = total
-
     if square:
-        arrived(q2_r.at[pl.ds(0, L - 1)], q2_in.at[0])
-
-    @pl.loop(0, L - 1)
-    def _(l):
-        if not square:
-            arrived(q_recv.at[pl.ds(1, C - 1), l], q_in.at[0 if square else l])
+        arrived(q2_r.at[pl.ds(0, L - 2)], q2_in.at[0])
+
+        @pl.loop(0, L - 2)
+        def _(l):
+            for i in range(2):
+                ing[l, :, cols(i)] += q2_r[l, i].astype(F32)
+
+    @pl.loop(L - 2 if square else 0, L)
+    def _(l):
+        arrived(q_recv.at[pl.ds(1, C - 1), l], q_in.at[l])
         for i in range(halves):
             total = ing[l, :, cols(i)]
-            if square:
-                total = total + q2_r[l, i].astype(F32)
-            else:
-                for d in range(1, C):
-                    total = total + q_recv[d, l, i].astype(F32)
+            for d in range(1, C):
+                total = total + q_recv[d, l, i].astype(F32)
             ing[l, :, cols(i)] = total
 
     @pl.loop(0, L)
     def _(l):
-        if square:
-            for copy in rs2_copies(l):
-                copy.wait_send()
-
-    @pl.loop(0, L - 1)
+        for copy in rs1_copies(l) + (rs2_copies(l) if square else []):
+            copy.wait_send()
+
+    @pl.loop(0, L - 2)
     def _(l):
         for copy in q1_copies(l) + q2_copies(l) if square else q_copies(l):
             copy.wait_send()
 
-    for copy in q_copies(L - 1):
+    for copy in q_copies(L - 2) + q_copies(L - 1):
         copy.wait_send()
 
 

time: 47.4 us -> 46.1 us (0.973)
  Pallas kernels: 46.6 us -> 45.3 us
    pallas_call x1, Pallas kernels: 45.6 us -> 44.3 us  [body(): pl.pallas_call(functools.partial(kernel, R, C), out_shape=(V((L, TC, KI),...]
where the time goes in v4:
time: 46.1 us; the launch traced here: 45.9 us
  Pallas kernels  45.3 us (98%)
  between operations  0.64 us (1%)
    pallas_call x1, Pallas kernels, body(): pl.pallas_call(functools.partial(kernel, R, C), out_shape=(V((L, TC, KI),...  44.3 us
    pallas_call x1, Pallas kernels, body(): pl.pallas_call(finish, out_shape=tuple((jax.ShapeDtypeStruct(x.shape, x.d...  0.98 us

profile of v4, /device:TPU:0, one launch (start us, length us, event | category | flops | bytes accessed | tf_op | source)
XLA Modules:
  0.0 45.9 jit_solution(10003172451606889533)
XLA Ops:
  0.6 44.3 %shard_map.93 = (bf16[6,128,256]{2,1,0:T(8,128)(2,1)S(1)}, f32[6,32,256]{2,1,0:T(8,128)S(1)}, f32[6,32,512]{2,1,0:T(8,128)S(1)}, f32[6,512]{1,0:T(8,128)S(1)}) custom-call(bf16[6,128,256]{2,1,0:T(8,128)(2,1)} %refs_0_.1, bf16[6,64,512]{2,1,0:T(8,128)(2,1)} %refs_1_.1, bf16[6,256,512]{2,1,0:T(8,128)(2,1)} %refs_2_.1, bf16[6,32,256]{2,1,0:T(8,128)(2,1)} %refs_3_.1, ...), custom_call_target="tpu_custom_call" | custom-call | tf_op jit(solution)/shard_map/pallas_call | solution.py:744
  45.0 1.0 %shard_map.94 = (bf16[6,128,256]{2,1,0:T(8,128)(2,1)}, f32[6,32,256]{2,1,0:T(8,128)}, f32[6,32,512]{2,1,0:T(8,128)}, f32[6,512]{1,0:T(8,128)}) custom-call(bf16[6,128,256]{2,1,0:T(8,128)(2,1)S(1)} %get-tuple-element.8.ig, f32[6,32,256]{2,1,0:T(8,128)S(1)} %get-tuple-element.9.ing, f32[6,32,512]{2,1,0:T(8,128)S(1)} %get-tuple-element.10.oug, ...), custom_call_target="tpu_custom_call" | custom-call | tf_op jit(solution)/shard_map/pallas_call | solution.py:754

commit v5 on v4

--- a/solution.py
+++ b/solution.py
@@ -39,7 +39,7 @@
         sqm=V((L, 1, W), F32), sq_sib=V((H, 1, W), F32), sq_z=V((Z, H, 1, W), F32), sq_tot=V((2, H, 1, W), F32),
         norms=V((L, 1, W), F32), scl=V((L, 1, W), F32), cor=V((L, 1, W), F32), mag3=V((L, 1, W), F32),
         mg3=V((L, 1, W), F32),
-        prod_buf=V((T, KI), F32), qs=V((2, H, RANK, TC), F32), q_sib=V((H, RANK, TC), F32), q_all=V((Z, H, RANK, TC), F32),
+        prod_buf=V((T, KI), F32), qs=V((2, H, RANK, TC), F32), q_sib=V((H, RANK, TC), F32), q_all=V((Z, H, RANK, TC), BF16),
         Qg=V((2, C, H, RANK, TC), BF16), Qc=V((L, RANK, T), BF16),
         ims=V((2, H, RANK, W), F32), im_sib=V((H, RANK, W), F32), im_all=V((Z, H, RANK, W), BF16),
         im_fin=V((2, H, RANK, W), BF16),
@@ -50,7 +50,7 @@
         rs2_s=V(slim, BF16), rs2_r=V(slim, BF16),
         send=dma((1,)), g_in=dma((L, Z - 1)), g_fw=dma((L,)), a_in=dma((L, 2)), rs1_in=dma((L,)), rs2_in=dma((1,)),
         sq_in=dma((1,)), dt_in=dma((2, L - 2)), dt_last=dma((2,)), root_in=dma((2,)), out_in=dma((2,)), col_in=dma((1,)),
-        sib_in=dma((6,)), news=pltpu.SemaphoreType.REGULAR((2, max(Z - 2, 1))), q_in=dma((L,)), q1_in=dma((L - 2,)), q2_in=dma((1,)),
+        sib_in=dma((6,)), news=pltpu.SemaphoreType.REGULAR((2, max(Z - 2, 1))), q_in=dma((2 if C == 4 else L,)), q1_in=dma((L - 2,)), q2_in=dma((1,)),
     )
 
 
@@ -266,9 +266,9 @@
         rcopy(im_fin.at[core], im_fin.at[core], sib_in.at[5], row=sib),
     ]
 
-    def root_copies():
-        return [rcopy(q_all.at[z], q_all.at[z], root_in.at[0], row=2 * root + core),
-                rcopy(im_all.at[z], im_all.at[z], root_in.at[1], row=2 * root + core)]
+    def root_copy(i):
+        ref = (q_all, im_all)[i].at[z]
+        return rcopy(ref, ref, root_in.at[i], row=2 * root + core)
 
     def out_ref(i):
         return Qg.at[core, c] if i == 0 else im_fin.at[core]
@@ -284,27 +284,26 @@
     def start(copy):
         copy.start()
 
-    def to_root():
-        arrived(q_sib, sib_in.at[2])
-        arrived(im_sib, sib_in.at[3])
-        q_all[z] = qs[core] + q_sib[...]
-        im_all[z] = (ims[core] + im_sib[...]).astype(BF16)
+    def to_root(i):
+        mine, theirs, every = (qs, q_sib, q_all) if i == 0 else (ims, im_sib, im_all)
+        arrived(theirs, sib_in.at[2 + i])
+        every[z] = (mine[core] + theirs[...]).astype(BF16)
 
         @pl.when(z != root)
         def _():
-            for copy in root_copies():
-                copy.start()
-
-    def at_root():
-        arrived(q_all.at[pl.ds(0, Z - 1)], root_in.at[0])
-        arrived(im_all.at[pl.ds(0, Z - 1)], root_in.at[1])
-        q_sum, im_sum = q_all[0], im_all[0].astype(F32)
+            root_copy(i).start()
+
+    def at_root(i):
+        every = (q_all, im_all)[i]
+        arrived(every.at[pl.ds(0, Z - 1)], root_in.at[i])
+        total = every[0].astype(F32)
         for s in range(1, Z):
-            q_sum = q_sum + q_all[s]
-            im_sum = im_sum + im_all[s].astype(F32)
-        Qg[core, c] = q_sum.astype(BF16)
-        im_fin[core] = im_sum.astype(BF16)
-        for copy in out_copies(0) + gather_copies():
+            total = total + every[s].astype(F32)
+        if i == 0:
+            Qg[core, c] = total.astype(BF16)
+        else:
+            im_fin[core] = total.astype(BF16)
+        for copy in out_copies(i) + (gather_copies() if i == 0 else [to_sib[5]]):
             copy.start()
 
     def q_arrived():
@@ -356,8 +355,11 @@
             dt_tot[l] = total
             dt_tot_copy(l).start()
 
+    def q_sem(l):
+        return q_in.at[l - (L - 2) if square else l]
+
     def q_copies(l):
-        return [rcopy(q.at[l], q_recv.at[d, l], q_in.at[l], col=col_to(d)) for d in range(1, C)]
+        return [rcopy(q.at[l], q_recv.at[d, l], q_sem(l), col=col_to(d)) for d in range(1, C)]
 
     def q1_copies(l):
         return [rcopy(q.at[l, i], q1_r.at[l, i], q1_in.at[l], col=to) for i, to in enumerate((xn, yn))]
@@ -435,42 +437,6 @@
             scl[l] = s
             ws[l] = (merged[l] * s).astype(BF16)
             asc[l] = (aout[l].astype(F32) * s).astype(BF16)
-
-    out = jnp.where(z < Z // 2, -1, 1)
-
-    def relay(at, d, step):
-        l = at - (d - 1)
-
-        @pl.when(jnp.logical_and(l >= 0, l < L))
-        def _():
-            g_relay(l, d, step, start, True)
-
-    def compute(l):
-        back = jnp.where(middle, 3, 2)
-
-        @pl.when(l >= back)
-        def _():
-            rs_second(l - back)
-
-        arrived(G.at[l, pl.ds(0, Z * TR)], g_fw.at[l])
-        a_ready(l)
-        g = G[l]
-        outer = mm(A[l], g, ((0,), (0,)))
-        dots_out(l, jnp.sum(merged[l] * outer, axis=0, keepdims=True))
-
-        @pl.when(jnp.logical_and(ends, l == L - 2))
-        def _():
-            relay(last - 1, Z - 2, out)
-
-        low = outer.astype(BF16)
-        prod_buf[...] = mm(g, ws[l], ((1,), (1,)))
-        rs_first(l, prod_buf)
-
-        @pl.when(jnp.logical_and(ends, l == L - 2))
-        def _():
-            relay(last, Z - 1, out)
-
-        ing[l] = mm(asc[l], low, ((1,), (1,)))
 
     def correct(l, direct):
         if isinstance(l, int) and l >= L - 2:
@@ -506,6 +472,56 @@
         for copy in q2_copies(l):
             copy.start()
 
+    out = jnp.where(z < Z // 2, -1, 1)
+
+    def relay(at, d, step):
+        l = at - (d - 1)
+
+        @pl.when(jnp.logical_and(l >= 0, l < L))
+        def _():
+            g_relay(l, d, step, start, True)
+
+    def compute(l):
+        back = jnp.where(middle, 3, 2)
+
+        @pl.when((l >= back) & (middle | (l < L - 1)))
+        def _():
+            rs_second(l - back)
+
+        @pl.when(jnp.logical_and(ends, l == L - 1))
+        def _():
+            correct(1, not square)
+            if square:
+                q_second(0)
+
+        arrived(G.at[l, pl.ds(0, Z * TR)], g_fw.at[l])
+        a_ready(l)
+        g = G[l]
+        outer = mm(A[l], g, ((0,), (0,)))
+        dots_out(l, jnp.sum(merged[l] * outer, axis=0, keepdims=True))
+
+        @pl.when(ends & (l == L - 2) & (core == 0))
+        def _():
+            relay(last - 1, Z - 2, out)
+
+        @pl.when(jnp.logical_and(ends, l == L - 1))
+        def _():
+            dots_sum(L - 3)
+
+        low = outer.astype(BF16)
+        prod_buf[...] = mm(g, ws[l], ((1,), (1,)))
+        rs_first(l, prod_buf)
+
+        @pl.when(ends & (l == L - 2) & (core == 0))
+        def _():
+            relay(last, Z - 1, out)
+
+        ing[l] = mm(asc[l], low, ((1,), (1,)))
+
+        @pl.when(jnp.logical_and(ends, l == L - 1))
+        def _():
+            rs_second(L - 3)
+
     def own_at(at):
         @pl.when(at + ahead < L)
         def _():
@@ -547,6 +563,11 @@
         def _():
             own_at(at)
             relay(at, Z - 1, out)
+
+        @pl.when(ends & (at == last - 1) & (core == 1))
+        def _():
+            relay(last - 1, Z - 2, out)
+            relay(last, Z - 1, out)
 
         if square:
             for l in (2 * at - 1, 2 * at):
@@ -560,11 +581,19 @@
 
         @pl.when(at == Z - 2)
         def _():
-            to_root()
-
-        @pl.when(jnp.logical_and(at == jnp.where(middle, last, last - 1), z != root))
+            to_root(1)
+
+        @pl.when(at == 0)
+        def _():
+            to_root(0)
+
+        @pl.when(jnp.logical_and(at == jnp.where(middle, last, last - 2), z != root))
         def _():
             q_arrived()
+
+        @pl.when(jnp.logical_and(at == Z - 2, z == root))
+        def _():
+            at_root(0)
 
         @pl.when(at == Z - 2)
         def _():
@@ -579,11 +608,7 @@
             for d in range(Z - 2, 0, -1):
                 relay(at, d, out)
 
-        @pl.when(jnp.logical_and(at == last - 4, z == root))
-        def _():
-            at_root()
-
-        @pl.when(jnp.logical_and(ends, at >= last - 3))
+        @pl.when(ends & (at >= last - 3) & (at < last))
         def _():
             dots_sum(at - (last - 3))
 
@@ -591,33 +616,32 @@
         def _():
             correct(0, not square)
 
+    def low_rank(half):
+        @pl.loop(0, H)
+        def _(at):
+            l = half * H + at
+            for s in range(C):
+                Qc[l, :, s * TC:(s + 1) * TC] = Qg[half, s, at]
+            oug[l] = mm(Qc[l], G[l], ((1,), (0,))) * scl[l]
+
     @pl.loop(jnp.where(middle, 0, L - 2), L - 2)
     def _(l):
         dots_sum(l)
 
-    @pl.loop(jnp.where(middle, 0, 1), L - 3)
+    @pl.loop(jnp.where(middle, 0, 2), L - 3)
     def _(l):
         correct(l, not square)
 
     @pl.when(z == root)
     def _():
-        for copy in out_copies(1):
-            copy.start()
-        to_sib[5].start()
+        at_root(1)
 
     arrived(Qg.at[core, pl.ds(0, C - 1)], col_in.at[0])
     to_sib[4].start()
 
     correct(L - 3, not square)
 
-    arrived(Qg.at[1 - core], sib_in.at[4])
-
-    @pl.loop(0, L)
-    def _(l):
-        half, at = l // H, lax.rem(l, H)
-        for s in range(C):
-            Qc[l, :, s * TC:(s + 1) * TC] = Qg[half, s, at]
-        oug[l] = mm(Qc[l], G[l], ((1,), (0,))) * scl[l]
+    low_rank(core)
 
     @pl.when(middle)
     def _():
@@ -627,12 +651,17 @@
 
     correct(L - 2, True)
 
+    if square:
+        @pl.loop(jnp.where(middle, 0, 1), 2)
+        def _(l):
+            q_second(l)
+
     correct(L - 1, True)
 
     rs_second(L - 1)
 
     if square:
-        @pl.loop(0, L - 2)
+        @pl.loop(2, L - 2)
         def _(l):
             q_second(l)
 
@@ -643,6 +672,9 @@
 
     for l in range(L):
         mgrad[l:l + 1] = mg3[l]
+
+    arrived(Qg.at[1 - core], sib_in.at[4])
+    low_rank(1 - core)
 
     arrived(im_fin.at[1 - core], sib_in.at[5])
 
@@ -683,8 +715,8 @@
 
     @pl.when(z != root)
     def _():
-        for copy in root_copies():
-            copy.wait_send()
+        root_copy(0).wait_send()
+        root_copy(1).wait_send()
 
     if square:
         arrived(rs2_r, rs2_in.at[0])
@@ -703,7 +735,7 @@
 
     @pl.loop(L - 2 if square else 0, L)
     def _(l):
-        arrived(q_recv.at[pl.ds(1, C - 1), l], q_in.at[l])
+        arrived(q_recv.at[pl.ds(1, C - 1), l], q_sem(l))
         for i in range(halves):
             total = ing[l, :, cols(i)]
             for d in range(1, C):

time: 46.1 us -> 45.4 us (0.985)
  Pallas kernels: 45.3 us -> 44.6 us
    pallas_call x1, Pallas kernels: 44.3 us -> 43.6 us  [body(): pl.pallas_call(functools.partial(kernel, R, C), out_shape=(V((L, TC, KI),...]
where the time goes in v5:
time: 45.4 us; the launch traced here: 45.2 us
  Pallas kernels  44.6 us (98%)
  between operations  0.64 us (1%)
    pallas_call x1, Pallas kernels, body(): pl.pallas_call(functools.partial(kernel, R, C), out_shape=(V((L, TC, KI),...  43.6 us
    pallas_call x1, Pallas kernels, body(): pl.pallas_call(finish, out_shape=tuple((jax.ShapeDtypeStruct(x.shape, x.d...  0.98 us

profile of v5, /device:TPU:0, one launch (start us, length us, event | category | flops | bytes accessed | tf_op | source)
XLA Modules:
  0.0 45.2 jit_solution(4825532314896379480)
XLA Ops:
  0.6 43.6 %shard_map.93 = (bf16[6,128,256]{2,1,0:T(8,128)(2,1)S(1)}, f32[6,32,256]{2,1,0:T(8,128)S(1)}, f32[6,32,512]{2,1,0:T(8,128)S(1)}, f32[6,512]{1,0:T(8,128)S(1)}) custom-call(bf16[6,128,256]{2,1,0:T(8,128)(2,1)} %refs_0_.1, bf16[6,64,512]{2,1,0:T(8,128)(2,1)} %refs_1_.1, bf16[6,256,512]{2,1,0:T(8,128)(2,1)} %refs_2_.1, bf16[6,32,256]{2,1,0:T(8,128)(2,1)} %refs_3_.1, ...), custom_call_target="tpu_custom_call" | custom-call | tf_op jit(solution)/shard_map/pallas_call | solution.py:776
  44.2 1.0 %shard_map.94 = (bf16[6,128,256]{2,1,0:T(8,128)(2,1)}, f32[6,32,256]{2,1,0:T(8,128)}, f32[6,32,512]{2,1,0:T(8,128)}, f32[6,512]{1,0:T(8,128)}) custom-call(bf16[6,128,256]{2,1,0:T(8,128)(2,1)S(1)} %get-tuple-element.8.ig, f32[6,32,256]{2,1,0:T(8,128)S(1)} %get-tuple-element.9.ing, f32[6,32,512]{2,1,0:T(8,128)S(1)} %get-tuple-element.10.oug, ...), custom_call_target="tpu_custom_call" | custom-call | tf_op jit(solution)/shard_map/pallas_call | solution.py:786

commit v6 on v5

--- a/solution.py
+++ b/solution.py
@@ -48,9 +48,9 @@
         q1_r=V(pair, BF16), q2_s=V(pair, BF16), q2_r=V(pair, BF16),
         own=V((L, TC, KI), F32), hold=V(slim, F32), rs1_s=V(wide, BF16), rs1_r=V(wide, BF16),
         rs2_s=V(slim, BF16), rs2_r=V(slim, BF16),
-        send=dma((1,)), g_in=dma((L, Z - 1)), g_fw=dma((L,)), a_in=dma((L, 2)), rs1_in=dma((L,)), rs2_in=dma((1,)),
+        send=dma((1,)), g_in=dma((L, Z - 1)), g_fw=dma((L + 1,)), a_in=dma((L, 2)), rs1_in=dma((L,)), rs2_in=dma((2,)),
         sq_in=dma((1,)), dt_in=dma((2, L - 2)), dt_last=dma((2,)), root_in=dma((2,)), out_in=dma((2,)), col_in=dma((1,)),
-        sib_in=dma((6,)), news=pltpu.SemaphoreType.REGULAR((2, max(Z - 2, 1))), q_in=dma((2 if C == 4 else L,)), q1_in=dma((L - 2,)), q2_in=dma((1,)),
+        sib_in=dma((6,)), news=pltpu.SemaphoreType.REGULAR((2, max(Z - 2, 1))), q_in=dma((2 if C == 4 else L,)), q1_in=dma((L - 2,)), q2_in=dma((2,)),
     )
 
 
@@ -80,6 +80,8 @@
     middle = jnp.logical_and(z > 0, z < Z - 1)
     ends = jnp.logical_not(middle)
     halves = 2 if square else 1
+    split = square and 2 * TR == TC
+    far = jnp.where(z < Z // 2, Z - 1, 0)
     KS = KI // halves
 
     def row_to(d):
@@ -152,6 +154,9 @@
     def g_sem(l, at, to):
         return g_in.at[l, at - jnp.where(at > to, 1, 0)]
 
+    def over(l, at):
+        return jnp.where(ends & (l == L - 2) & (at == far), L, l) if split else l
+
     def g_own(l, step):
         if step == 0:
             return rcopy(grads.at[l], g_block(l, z, core), g_fw.at[l], row=sib)
@@ -160,7 +165,7 @@
     def g_pass(l, at, step):
         block = g_block(l, at, core)
         if isinstance(step, int) and step == 0:
-            return rcopy(block, block, g_fw.at[l], row=sib)
+            return rcopy(block, block, g_fw.at[over(l, at)], row=sib)
         return rcopy(block, block, g_sem(l, at, z + step), row=r + 2 * step)
 
     def g_own_each(l, act):
@@ -219,7 +224,21 @@
         return [rcopy(rs1_s.at[d, l], rs1_r.at[d, l], rs1_in.at[l], col=col_to(d)) for d in range(1, C)]
 
     def rs2_copies(l):
-        return [rcopy(rs2_s.at[i, l], rs2_r.at[i, l], rs2_in.at[0], col=to) for i, to in enumerate((yn, xn))]
+        return [rcopy(rs2_s.at[i, l], rs2_r.at[i, l], rs2_in.at[l // (L - 1)], col=to) for i, to in enumerate((yn, xn))]
+
+    def rs_keep(l, prod):
+        for i in range(2):
+            hold[i, l] = prod[rows((yn, xn)[i], TC), cols(i)]
+        own[l] = prod[rows(c, TC)]
+
+    def rs_parts(l, late):
+        for i, near in enumerate((xn, yn)):
+            for which, block in enumerate((near, dg)):
+                @pl.when((block == far) if late else (block != far))
+                def _():
+                    part, there = rs1_s.at[i, l, which], rs1_r.at[i, l, which]
+                    rs1_s[i, l, which] = prod_buf[rows(block, TC), cols(i)].astype(BF16)
+                    rcopy(part, there, rs1_in.at[l], col=near).start()
 
     def rs_first(l, prod):
         if square:
@@ -365,7 +384,7 @@
         return [rcopy(q.at[l, i], q1_r.at[l, i], q1_in.at[l], col=to) for i, to in enumerate((xn, yn))]
 
     def q2_copies(l):
-        return [rcopy(q2_s.at[l, i], q2_r.at[l, i], q2_in.at[0], col=to) for i, to in enumerate((yn, xn))]
+        return [rcopy(q2_s.at[l, i], q2_r.at[l, i], q2_in.at[l // (L - 3)], col=to) for i, to in enumerate((yn, xn))]
 
     def cols(i):
         return slice(i * KS, (i + 1) * KS)
@@ -488,13 +507,20 @@
         def _():
             rs_second(l - back)
 
-        @pl.when(jnp.logical_and(ends, l == L - 1))
-        def _():
-            correct(1, not square)
-            if square:
-                q_second(0)
-
-        arrived(G.at[l, pl.ds(0, Z * TR)], g_fw.at[l])
+        if split:
+            @pl.when(jnp.logical_or(middle, l != L - 2))
+            def _():
+                arrived(G.at[l, pl.ds(0, Z * TR)], g_fw.at[l])
+
+            @pl.when(jnp.logical_and(ends, l == L - 2))
+            def _():
+                arrived(G.at[l, pl.ds(0, (Z - 1) * TR)], g_fw.at[l])
+                near_rows = pl.ds(pl.multiple_of(jnp.where(far == 0, TC, 0), TC), (Z - 1) * TC)
+                prod_buf[near_rows] = mm(G[l, near_rows], ws[l], ((1,), (1,)))
+                rs_parts(l, False)
+                arrived(G.at[l, pl.ds(0, TR)], g_fw.at[L])
+        else:
+            arrived(G.at[l, pl.ds(0, Z * TR)], g_fw.at[l])
         a_ready(l)
         g = G[l]
         outer = mm(A[l], g, ((0,), (0,)))
@@ -504,13 +530,30 @@
         def _():
             relay(last - 1, Z - 2, out)
 
+        @pl.when(jnp.logical_and(ends, l == L - 2))
+        def _():
+            dots_sum(L - 4)
+            correct(1, not square)
+
         @pl.when(jnp.logical_and(ends, l == L - 1))
         def _():
             dots_sum(L - 3)
 
         low = outer.astype(BF16)
-        prod_buf[...] = mm(g, ws[l], ((1,), (1,)))
-        rs_first(l, prod_buf)
+        if split:
+            @pl.when(jnp.logical_or(middle, l != L - 2))
+            def _():
+                prod_buf[...] = mm(G[l], ws[l], ((1,), (1,)))
+                rs_first(l, prod_buf)
+
+            @pl.when(jnp.logical_and(ends, l == L - 2))
+            def _():
+                prod_buf[rows(far, TC)] = mm(G[l, rows(far, TC)], ws[l], ((1,), (1,)))
+                rs_parts(l, True)
+                rs_keep(l, prod_buf)
+        else:
+            prod_buf[...] = mm(g, ws[l], ((1,), (1,)))
+            rs_first(l, prod_buf)
 
         @pl.when(ends & (l == L - 2) & (core == 0))
         def _():
@@ -608,7 +651,7 @@
             for d in range(Z - 2, 0, -1):
                 relay(at, d, out)
 
-        @pl.when(ends & (at >= last - 3) & (at < last))
+        @pl.when(ends & (at >= last - 3) & (at < last - 1))
         def _():
             dots_sum(at - (last - 3))
 
@@ -652,16 +695,14 @@
     correct(L - 2, True)
 
     if square:
-        @pl.loop(jnp.where(middle, 0, 1), 2)
-        def _(l):
-            q_second(l)
+        q_second(0)
 
     correct(L - 1, True)
 
     rs_second(L - 1)
 
     if square:
-        @pl.loop(2, L - 2)
+        @pl.loop(1, L - 2)
         def _(l):
             q_second(l)
 
@@ -718,29 +759,46 @@
         root_copy(0).wait_send()
         root_copy(1).wait_send()
 
-    if square:
-        arrived(rs2_r, rs2_in.at[0])
-
-    @pl.loop(0, L)
-    def _(l):
-        rs_finish(l)
-
-    if square:
-        arrived(q2_r.at[pl.ds(0, L - 2)], q2_in.at[0])
-
-        @pl.loop(0, L - 2)
-        def _(l):
-            for i in range(2):
-                ing[l, :, cols(i)] += q2_r[l, i].astype(F32)
-
-    @pl.loop(L - 2 if square else 0, L)
-    def _(l):
+    def q_finish(l):
         arrived(q_recv.at[pl.ds(1, C - 1), l], q_sem(l))
         for i in range(halves):
             total = ing[l, :, cols(i)]
             for d in range(1, C):
                 total = total + q_recv[d, l, i].astype(F32)
             ing[l, :, cols(i)] = total
+
+    def q2_finish(l):
+        for i in range(2):
+            ing[l, :, cols(i)] += q2_r[l, i].astype(F32)
+
+    if square:
+        arrived(rs2_r.at[:, pl.ds(0, L - 1)], rs2_in.at[0])
+
+    @pl.loop(0, L - 1)
+    def _(l):
+        rs_finish(l)
+
+    if square:
+        arrived(q2_r.at[pl.ds(0, L - 3)], q2_in.at[0])
+
+        @pl.loop(0, L - 3)
+        def _(l):
+            q2_finish(l)
+
+        q_finish(L - 2)
+    else:
+        @pl.loop(0, L - 1)
+        def _(l):
+            q_finish(l)
+
+    if square:
+        arrived(rs2_r.at[:, L - 1], rs2_in.at[1])
+    rs_finish(L - 1)
+
+    q_finish(L - 1)
+    if square:
+        arrived(q2_r.at[L - 3], q2_in.at[1])
+        q2_finish(L - 3)
 
     @pl.loop(0, L)
     def _(l):

time: 45.4 us -> 44.9 us (0.989)
  Pallas kernels: 44.6 us -> 44.1 us
where the time goes in v6:
time: 44.9 us; the launch traced here: 44.8 us
  Pallas kernels  44.1 us (98%)
  between operations  0.64 us (1%)
    pallas_call x1, Pallas kernels, body(): pl.pallas_call(functools.partial(kernel, R, C), out_shape=(V((L, TC, KI),...  43.1 us
    pallas_call x1, Pallas kernels, body(): pl.pallas_call(finish, out_shape=tuple((jax.ShapeDtypeStruct(x.shape, x.d...  0.98 us

profile of v6, /device:TPU:0, one launch (start us, length us, event | category | flops | bytes accessed | tf_op | source)
XLA Modules:
  0.0 44.8 jit_solution(6776879169638253653)
XLA Ops:
  0.6 43.1 %shard_map.93 = (bf16[6,128,256]{2,1,0:T(8,128)(2,1)S(1)}, f32[6,32,256]{2,1,0:T(8,128)S(1)}, f32[6,32,512]{2,1,0:T(8,128)S(1)}, f32[6,512]{1,0:T(8,128)S(1)}) custom-call(bf16[6,128,256]{2,1,0:T(8,128)(2,1)} %refs_0_.1, bf16[6,64,512]{2,1,0:T(8,128)(2,1)} %refs_1_.1, bf16[6,256,512]{2,1,0:T(8,128)(2,1)} %refs_2_.1, bf16[6,32,256]{2,1,0:T(8,128)(2,1)} %refs_3_.1, ...), custom_call_target="tpu_custom_call" | custom-call | tf_op jit(solution)/shard_map/pallas_call | solution.py:834
  43.8 1.0 %shard_map.94 = (bf16[6,128,256]{2,1,0:T(8,128)(2,1)}, f32[6,32,256]{2,1,0:T(8,128)}, f32[6,32,512]{2,1,0:T(8,128)}, f32[6,512]{1,0:T(8,128)}) custom-call(bf16[6,128,256]{2,1,0:T(8,128)(2,1)S(1)} %get-tuple-element.8.ig, f32[6,32,256]{2,1,0:T(8,128)S(1)} %get-tuple-element.9.ing, f32[6,32,512]{2,1,0:T(8,128)S(1)} %get-tuple-element.10.oug, ...), custom_call_target="tpu_custom_call" | custom-call | tf_op jit(solution)/shard_map/pallas_call | solution.py:844

commit v7 on v6

--- a/solution.py
+++ b/solution.py
@@ -17,7 +17,7 @@
 
 
 NAMES = (
-    "acts", "grads", "frozen", "ain", "aout", "mag", "load", "G", "A", "merged", "ws", "asc", "sqm", "sq_sib", "sq_z",
+    "acts", "grads", "frozen", "ain", "aout", "mag", "load", "G", "A", "AT", "merged", "ws", "asc", "sqm", "sq_sib", "sq_z",
     "sq_tot", "norms", "scl", "cor", "mag3", "mg3", "prod_buf", "qs", "q_sib", "q_all", "Qg", "Qc", "ims", "im_sib",
     "im_all", "im_fin", "dt_own", "dt_tot", "dt_all", "q", "q_recv", "q1_r", "q2_s", "q2_r", "own",
     "hold", "rs1_s", "rs1_r", "rs2_s", "rs2_r", "send", "g_in", "g_fw", "a_in", "rs1_in", "rs2_in", "sq_in", "dt_in",
@@ -34,7 +34,7 @@
     return dict(
         acts=V((L, TC, KI), BF16), grads=V((L, TR, W), BF16), frozen=V((L, KI, W), BF16),
         ain=V((L, RANK, KI), BF16), aout=V((L, RANK, W), BF16), mag=V((L, W), F32), load=dma((6,)),
-        G=V((L, T, W), BF16), A=V((L, T, KI), BF16), merged=V((L, KI, W), F32), ws=V((L, KI, W), BF16),
+        G=V((L, T, W), BF16), A=V((L, T, KI), BF16), AT=V((L, KI, T), BF16), merged=V((L, KI, W), F32), ws=V((L, KI, W), BF16),
         asc=V((L, RANK, W), BF16),
         sqm=V((L, 1, W), F32), sq_sib=V((H, 1, W), F32), sq_z=V((Z, H, 1, W), F32), sq_tot=V((2, H, 1, W), F32),
         norms=V((L, 1, W), F32), scl=V((L, 1, W), F32), cor=V((L, 1, W), F32), mag3=V((L, 1, W), F32),
@@ -56,7 +56,7 @@
 
 def kernel(R, C, *refs):
     acts_hbm, grads_hbm, frozen_hbm, ain_hbm, aout_hbm, mag_hbm, ig, ing, oug, mgrad = refs[:10]
-    (acts, grads, frozen, ain, aout, mag, load, G, A, merged, ws, asc, sqm, sq_sib, sq_z, sq_tot, norms, scl, cor,
+    (acts, grads, frozen, ain, aout, mag, load, G, A, AT, merged, ws, asc, sqm, sq_sib, sq_z, sq_tot, norms, scl, cor,
      mag3, mg3, prod_buf, qs, q_sib, q_all, Qg, Qc, ims, im_sib, im_all, im_fin, dt_own, dt_tot,
      dt_all, q, q_recv, q1_r, q2_s, q2_r, own, hold, rs1_s, rs1_r, rs2_s, rs2_r, send, g_in, g_fw, a_in, rs1_in,
      rs2_in, sq_in, dt_in, dt_last, root_in, out_in, col_in, sib_in, news, q_in, q1_in, q2_in) = refs[10:]
@@ -500,7 +500,15 @@
         def _():
             g_relay(l, d, step, start, True)
 
+    def turn(l):
+        a_ready(l)
+        AT[l] = A[l].T
+
     def compute(l):
+        @pl.when(l < L - 1)
+        def _():
+            turn(l + 1)
+
         back = jnp.where(middle, 3, 2)
 
         @pl.when((l >= back) & (middle | (l < L - 1)))
@@ -521,9 +529,8 @@
                 arrived(G.at[l, pl.ds(0, TR)], g_fw.at[L])
         else:
             arrived(G.at[l, pl.ds(0, Z * TR)], g_fw.at[l])
-        a_ready(l)
         g = G[l]
-        outer = mm(A[l], g, ((0,), (0,)))
+        outer = mm(AT[l], g, ((1,), (0,)))
         dots_out(l, jnp.sum(merged[l] * outer, axis=0, keepdims=True))
 
         @pl.when(ends & (l == L - 2) & (core == 0))
@@ -559,11 +566,11 @@
         def _():
             relay(last, Z - 1, out)
 
+        @pl.when(jnp.logical_and(ends, l == L - 1))
+        def _():
+            rs_second(L - 3)
+
         ing[l] = mm(asc[l], low, ((1,), (1,)))
-
-        @pl.when(jnp.logical_and(ends, l == L - 1))
-        def _():
-            rs_second(L - 3)
 
     def own_at(at):
         @pl.when(at + ahead < L)
@@ -641,6 +648,7 @@
         @pl.when(at == Z - 2)
         def _():
             scales()
+            turn(0)
 
         @pl.when(at >= Z - 2)
         def _():

time: 44.9 us -> 44.9 us (level)
  no operation moved by 1% of the time
where the time goes in v7:
time: 44.9 us; the launch traced here: 44.8 us
  Pallas kernels  44.1 us (98%)
  between operations  0.64 us (1%)
    pallas_call x1, Pallas kernels, body(): pl.pallas_call(functools.partial(kernel, R, C), out_shape=(V((L, TC, KI),...  43.1 us
    pallas_call x1, Pallas kernels, body(): pl.pallas_call(finish, out_shape=tuple((jax.ShapeDtypeStruct(x.shape, x.d...  0.98 us

profile of v7, /device:TPU:0, one launch (start us, length us, event | category | flops | bytes accessed | tf_op | source)
XLA Modules:
  0.0 44.8 jit_solution(6591944137665258066)
XLA Ops:
  0.6 43.1 %shard_map.93 = (bf16[6,128,256]{2,1,0:T(8,128)(2,1)S(1)}, f32[6,32,256]{2,1,0:T(8,128)S(1)}, f32[6,32,512]{2,1,0:T(8,128)S(1)}, f32[6,512]{1,0:T(8,128)S(1)}) custom-call(bf16[6,128,256]{2,1,0:T(8,128)(2,1)} %refs_0_.1, bf16[6,64,512]{2,1,0:T(8,128)(2,1)} %refs_1_.1, bf16[6,256,512]{2,1,0:T(8,128)(2,1)} %refs_2_.1, bf16[6,32,256]{2,1,0:T(8,128)(2,1)} %refs_3_.1, ...), custom_call_target="tpu_custom_call" | custom-call | tf_op jit(solution)/shard_map/pallas_call | solution.py:842
  43.8 1.0 %shard_map.94 = (bf16[6,128,256]{2,1,0:T(8,128)(2,1)}, f32[6,32,256]{2,1,0:T(8,128)}, f32[6,32,512]{2,1,0:T(8,128)}, f32[6,512]{1,0:T(8,128)}) custom-call(bf16[6,128,256]{2,1,0:T(8,128)(2,1)S(1)} %get-tuple-element.8.ig, f32[6,32,256]{2,1,0:T(8,128)S(1)} %get-tuple-element.9.ing, f32[6,32,512]{2,1,0:T(8,128)S(1)} %get-tuple-element.10.oug, ...), custom_call_target="tpu_custom_call" | custom-call | tf_op jit(solution)/shard_map/pallas_call | solution.py:852

commit v8 on v7

--- a/solution.py
+++ b/solution.py
@@ -690,9 +690,9 @@
     arrived(Qg.at[core, pl.ds(0, C - 1)], col_in.at[0])
     to_sib[4].start()
 
+    low_rank(core)
+
     correct(L - 3, not square)
-
-    low_rank(core)
 
     @pl.when(middle)
     def _():

time: 44.9 us -> 44.9 us (level)
  no operation moved by 1% of the time
where the time goes in v8:
time: 44.9 us; the launch traced here: 44.8 us
  Pallas kernels  44.1 us (98%)
  between operations  0.64 us (1%)
    pallas_call x1, Pallas kernels, body(): pl.pallas_call(functools.partial(kernel, R, C), out_shape=(V((L, TC, KI),...  43.1 us
    pallas_call x1, Pallas kernels, body(): pl.pallas_call(finish, out_shape=tuple((jax.ShapeDtypeStruct(x.shape, x.d...  0.98 us

profile of v8, /device:TPU:0, one launch (start us, length us, event | category | flops | bytes accessed | tf_op | source)
XLA Modules:
  0.0 44.8 jit_solution(855351717196105489)
XLA Ops:
  0.6 43.1 %shard_map.93 = (bf16[6,128,256]{2,1,0:T(8,128)(2,1)S(1)}, f32[6,32,256]{2,1,0:T(8,128)S(1)}, f32[6,32,512]{2,1,0:T(8,128)S(1)}, f32[6,512]{1,0:T(8,128)S(1)}) custom-call(bf16[6,128,256]{2,1,0:T(8,128)(2,1)} %refs_0_.1, bf16[6,64,512]{2,1,0:T(8,128)(2,1)} %refs_1_.1, bf16[6,256,512]{2,1,0:T(8,128)(2,1)} %refs_2_.1, bf16[6,32,256]{2,1,0:T(8,128)(2,1)} %refs_3_.1, ...), custom_call_target="tpu_custom_call" | custom-call | tf_op jit(solution)/shard_map/pallas_call | solution.py:842
  43.8 1.0 %shard_map.94 = (bf16[6,128,256]{2,1,0:T(8,128)(2,1)}, f32[6,32,256]{2,1,0:T(8,128)}, f32[6,32,512]{2,1,0:T(8,128)}, f32[6,512]{1,0:T(8,128)}) custom-call(bf16[6,128,256]{2,1,0:T(8,128)(2,1)S(1)} %get-tuple-element.8.ig, f32[6,32,256]{2,1,0:T(8,128)S(1)} %get-tuple-element.9.ing, f32[6,32,512]{2,1,0:T(8,128)S(1)} %get-tuple-element.10.oug, ...), custom_call_target="tpu_custom_call" | custom-call | tf_op jit(solution)/shard_map/pallas_call | solution.py:852
